TPU v7x, 32 devices: a whole 2x2x4 slice. The times are simulated.
32 devices in a mesh: gx: 2 (over x), gy: 4 (over y, core), gz: 4 (over z).
Axes of the slice: x: 2, y: 2, z: 4, core: 2. Of those that a mesh axis runs over, the one named last changes fastest.
Arguments:
- ambient_motion_array: float32 [3, 16, 256, 512], P(None, 'gx', 'gy', 'gz'), may hold values from -6 to 6
- ambient_scalar_trio: float32 [3, 16, 256, 512], P(None, 'gx', 'gy', 'gz'), may hold values from 0.2 to 1
- droplet_local_position: float32 [3, 32768], P(None, ('gx', 'gy', 'gz')), may hold values from -0.5 to 0.5
- droplet_motion_array: float32 [3, 32768], P(None, ('gx', 'gy', 'gz')), may hold values from -6 to 6
- droplet_heat_level: float32 [32768], P(('gx', 'gy', 'gz')), may hold values from 0.3 to 0.9
- droplet_size_quadratic: float32 [32768], P(('gx', 'gy', 'gz')), may hold values from 0.25 to 4
- local_i_position: int32 [32768], P(('gx', 'gy', 'gz')), may hold values from 0 to 7
- local_j_position: int32 [32768], P(('gx', 'gy', 'gz')), may hold values from 0 to 63
- local_k_position: int32 [32768], P(('gx', 'gy', 'gz')), may hold values from 0 to 127
- active_group_tally: int32 [32], P(('gx', 'gy', 'gz')), may hold values from 1 to 8, as said below
Outputs:
- gas_source: float32 [5, 16, 256, 512], P(None, 'gx', 'gy', 'gz')
- parcel_state: float32 [5, 32768], P(None, ('gx', 'gy', 'gz'))
Inputs may be any that keep to these rules, and one draw needn't show every extreme that they name: `active_group_tally`: tiles of a brick are live from the first one on; in every draw some brick has all 8 tiles live.
All inputs are finite; a program needn't handle non-finite values.
Results may differ from a plain program's by a relative error of at most 0.0003.
Values sent between devices are 32-bit elements; how exact they have to be, the bound alone decides.
A program may use at most 128 MiB of HBM per device.

v0:
```python
import functools

import jax
import jax.numpy as jnp
from jax import lax
from jax.experimental import pallas as pl
from jax.experimental.pallas import tpu as pltpu
from jax.sharding import PartitionSpec as P

TILE = 128
AXES = ("gx", "gy", "gz")
MESH = pl.DeviceIdType.MESH
F32 = jnp.float32
BF16 = jnp.bfloat16

step_time = 0.25
evap_rate = 1.0
heat_rate = 2.0
boiling_energy_drain = 0.3

X_MOVES = ((1, 0, 0, 0), (-1, 0, 0, 1))
Y_MOVES = ((0, 1, 0, 0), (0, -1, 0, 1))
XY_MOVES = ((1, 1, 0, 0), (1, -1, 0, 1), (-1, 1, 0, 2), (-1, -1, 0, 3))
Z_MOVES = ((0, 0, 1, 0), (0, 0, -1, 1))


def split(value):
    high = value.astype(BF16)
    return high, (value - high.astype(F32)).astype(BF16)


def nn(a, b):
    return lax.dot_general(a, b, (((1,), (0,)), ((), ())), preferred_element_type=F32)


def nt(a, b):
    return lax.dot_general(a, b, (((1,), (1,)), ((), ())), preferred_element_type=F32)


def tn(a, b):
    return lax.dot_general(a, b, (((0,), (0,)), ((), ())), preferred_element_type=F32)


def pair_weights(offset):
    lower = jnp.where(offset < 0.0, -1.0, 0.0)
    first = jnp.maximum(0.0, 1.0 - jnp.abs(offset - lower))
    second = jnp.maximum(0.0, 1.0 - jnp.abs(offset - (lower + 1.0)))
    return first, second, jnp.where(offset < 0.0, -1, 0)


def kernel(
    counts,
    vel,
    sca,
    pos,
    mot,
    heat,
    size,
    li,
    lj,
    lk,
    tally,
    dep,
    state,
    fields,
    ft_hi,
    ft_lo,
    w_hi,
    w_lo,
    line,
    src_hi,
    src_lo,
    sampled,
    xh,
    yh,
    xyh,
    zh,
    ys,
    xys,
    zs,
    dxs,
    dys,
    dxys,
    dzs,
    dxr,
    dyr,
    dxyr,
    dzr,
    load_sem,
    send_sem,
    recv_sem,
):
    ci, cj, ck = vel.shape[1:]
    slots = heat.shape[1]
    inner = ci * cj
    planes = w_hi.shape[0]
    outer = planes - inner
    y_row = 2 * cj
    xy_row = y_row + 2 * ci
    me = [lax.axis_index(axis) for axis in AXES]

    def exists(move, sign):
        good = None
        for d in range(3):
            step = sign * move[d]
            if step == 1:
                test = me[d] < counts[d] - 1
            elif step == -1:
                test = me[d] > 0
            else:
                continue
            good = test if good is None else jnp.logical_and(good, test)
        return good

    def peer(move):
        return tuple(lax.rem(me[d] + move[d] + counts[d], counts[d]) for d in range(3))

    moves = X_MOVES + Y_MOVES + XY_MOVES + Z_MOVES

    class Message:
        def __init__(self, number, move, src, dst):
            self.move = move
            self.dst = dst
            self.copy = pltpu.make_async_remote_copy(
                src_ref=src,
                dst_ref=dst,
                send_sem=send_sem.at[number],
                recv_sem=recv_sem.at[number],
                device_id=peer(move),
                device_id_type=MESH,
            )

        def start(self):
            @pl.when(exists(self.move, 1))
            def _():
                self.copy.start()

        def blank(self):
            @pl.when(jnp.logical_not(exists(self.move, -1)))
            def _():
                self.dst[...] = jnp.zeros(self.dst.shape, F32)

        def arrive(self):
            @pl.when(exists(self.move, -1))
            def _():
                self.copy.wait_recv()

        def leave(self):
            @pl.when(exists(self.move, 1))
            def _():
                self.copy.wait_send()

    x_in, y_in, z_in, x_out, xy_out, z_out = [], [], [], [], [], []
    number = 0

    def add(group, move, src, dst):
        nonlocal number
        group.append(Message(number, move, src, dst))
        number += 1

    for move in X_MOVES:
        row = ci - 1 if move[0] > 0 else 0
        add(x_in, move, vel.at[:, row], xh.at[move[3], 0:3])
        add(x_in, move, sca.at[:, row], xh.at[move[3], 3:6])
    for move in Y_MOVES:
        add(y_in, move, ys.at[move[3]], yh.at[move[3]])
    for move in XY_MOVES:
        add(y_in, move, xys.at[move[3]], xyh.at[move[3]])
    for move in Z_MOVES:
        add(z_in, move, zs.at[move[3]], zh.at[move[3]])
    for move in Z_MOVES:
        add(z_out, move, dzs.at[move[3]], dzr.at[move[3]])
    for move in X_MOVES:
        add(x_out, move, dxs.at[move[3]], dxr.at[move[3]])
    for move in Y_MOVES:
        add(xy_out, move, dys.at[move[3]], dyr.at[move[3]])
    for move in XY_MOVES:
        add(xy_out, move, dxys.at[move[3]], dxyr.at[move[3]])

    barrier = pltpu.get_barrier_semaphore()
    for move in moves:

        @pl.when(exists(move, 1))
        def _():
            pl.semaphore_signal(barrier, inc=1, device_id=peer(move), device_id_type=MESH)

    loads = [
        pltpu.make_async_copy(vel, fields.at[0:3], load_sem.at[0]),
        pltpu.make_async_copy(sca, fields.at[3:6], load_sem.at[1]),
    ]
    for load in loads:
        load.start()
    for message in x_in + y_in + z_in + z_out + x_out + xy_out:
        message.blank()

    pl.semaphore_wait(barrier, sum(exists(move, 1).astype(jnp.int32) for move in moves))

    for message in x_in:
        message.start()
    for load in loads:
        load.wait()

    for s in range(2):
        row = cj - 1 if s == 0 else 0
        ys[s] = fields[:, :, row, :]
        for t in range(2):
            plane = ci - 1 if t == 0 else 0
            xys[t * 2 + s] = jnp.concatenate(
                [fields[:, plane, row, :], jnp.zeros((2, ck), F32)], axis=0
            )
    for message in y_in:
        message.start()

    xa, xb, lx = pair_weights(pos[0:1])
    ya, yb, ly = pair_weights(pos[1:2])
    za, zb, lz = pair_weights(pos[2:3])
    i0 = li[...] + lx
    j0 = lj[...] + ly
    k0 = lk[...] + lz
    codes = []
    for a, wa in enumerate((xa, xb)):
        for b, wb in enumerate((ya, yb)):
            i, j = i0 + a, j0 + b
            out_i = (i < 0) | (i >= ci)
            out_j = (j < 0) | (j >= cj)
            si = jnp.where(i < 0, 0, 1)
            sj = jnp.where(j < 0, 0, 1)
            code = jnp.where(
                out_i,
                jnp.where(out_j, inner + xy_row + si * 2 + sj, inner + si * cj + j),
                jnp.where(out_j, inner + y_row + sj * ci + i, i * cj + j),
            )
            codes.append((code, wa * wb))
    block = 128
    for start in range(0, planes, block):
        rows = lax.broadcasted_iota(jnp.int32, (block, slots), 0) + start
        table = jnp.zeros((block, slots), F32)
        for code, weight in codes:
            table = jnp.where(rows == code, weight, table)
        high, low = split(table)
        w_hi[start : start + block] = high
        w_lo[start : start + block] = low
    lines = lax.broadcasted_iota(jnp.int32, (ck, slots), 0)
    line[...] = jnp.where(lines == k0, za, jnp.where(lines == k0 + 1, zb, 0.0))
    rim = (jnp.where(k0 < 0, za, 0.0), jnp.where(k0 + 1 >= ck, zb, 0.0))

    zs[...] = jnp.zeros_like(zs)

    def lay(f, first, flat):
        wide = flat.shape[0]
        turned = flat.T
        high, low = split(turned)
        ft_hi[f * ck : (f + 1) * ck, first : first + wide] = high
        ft_lo[f * ck : (f + 1) * ck, first : first + wide] = low
        zs[0, f : f + 1, first : first + wide] = turned[ck - 1 : ck]
        zs[1, f : f + 1, first : first + wide] = turned[0:1]

    for f in range(6):
        lay(f, 0, fields[f].reshape(inner, ck))

    width = 256

    def sample(first, last, fresh):
        for s in range(0, slots, width):
            here = slice(s, s + width)
            got = nn(ft_hi[:, first:last], w_hi[first:last, here])
            got += nn(ft_hi[:, first:last], w_lo[first:last, here])
            got += nn(ft_lo[:, first:last], w_hi[first:last, here])
            for f in range(6):
                part = jnp.sum(
                    got[f * ck : (f + 1) * ck] * line[:, here], axis=0, keepdims=True
                )
                if fresh:
                    sampled[f : f + 1, here] = part
                else:
                    sampled[f : f + 1, here] += part

    sample(0, inner, True)

    for message in x_in + y_in:
        message.arrive()
    for f in range(6):
        flat = jnp.concatenate(
            [xh[0, f], xh[1, f], yh[0, f], yh[1, f]]
            + [xyh[q, f : f + 1] for q in range(4)]
            + [jnp.zeros((outer - xy_row - 4, ck), F32)],
            axis=0,
        )
        lay(f, inner, flat)
    for message in z_in:
        message.start()
    sample(inner, planes, False)
    for message in z_in:
        message.arrive()
    ends = jnp.concatenate([zh[0], zh[1]], axis=0)
    end_hi, end_lo = split(ends)
    got = nn(end_hi, w_hi[...]) + nn(end_hi, w_lo[...]) + nn(end_lo, w_hi[...])
    gas = sampled[...] + got[0:8] * rim[0] + got[8:16] * rim[1]

    live = lax.broadcasted_iota(jnp.int32, (1, slots), 1) // TILE < tally[0]
    q = size[...]
    tp = heat[...]
    v = mot[...]
    drag = step_time / (0.5 * q)
    v_new = (v + drag * gas[0:3]) / (1.0 + drag)
    mass = q * jnp.sqrt(q)
    share = jnp.exp(4.0 * (tp - 1.0))
    decay = step_time * evap_rate * gas[5:6] * (share - gas[4:5])
    q_new = q - decay
    mass_new = q_new * jnp.sqrt(q_new)
    conduct = step_time * heat_rate * gas[5:6] / q
    tp_new = (tp + conduct * gas[3:4]) / (1.0 + conduct) - boiling_energy_drain * decay / q
    state[0:3] = jnp.where(live, v_new, v)
    state[3:4] = jnp.where(live, tp_new, tp)
    state[4:5] = jnp.where(live, q_new, q)
    push = jnp.where(live, mass * (v - v_new), 0.0)
    terms = [
        push[0:1],
        push[1:2],
        push[2:3],
        jnp.where(live, mass * (tp - tp_new), 0.0),
        jnp.where(live, mass - mass_new, 0.0),
    ]
    stack = jnp.concatenate(terms + [jnp.zeros((3, slots), F32)], axis=0)
    ends = jnp.concatenate([stack * rim[1], stack * rim[0]], axis=0)
    end_hi, end_lo = split(ends)
    got = nt(end_hi, w_hi[...]) + nt(end_hi, w_lo[...]) + nt(end_lo, w_hi[...])
    dzs[0] = got[0:8]
    dzs[1] = got[8:16]
    for message in z_out:
        message.start()

    for c in range(5):
        high, low = split(line[...] * terms[c])
        src_hi[c * ck : (c + 1) * ck] = high
        src_lo[c * ck : (c + 1) * ck] = low

    def spread(first, last, low, high):
        got = nt(w_hi[first:last], src_hi[low:high])
        got += nt(w_hi[first:last], src_lo[low:high])
        got += nt(w_lo[first:last], src_hi[low:high])
        return got

    pick_row = lax.broadcasted_iota(jnp.int32, (32, 5 * ck), 0)
    pick_col = lax.broadcasted_iota(jnp.int32, (32, 5 * ck), 1)
    pick_row = jnp.where(pick_row >= 16, pick_row - 16, pick_row)
    target = jnp.where(pick_row >= 8, (pick_row - 8) * ck + ck - 1, pick_row * ck)
    pick = jnp.where(target == pick_col, 1.0, 0.0).astype(BF16)

    spans = [(c, min(c + 2, 5)) for c in range(0, 5, 2)]
    halo = [spread(inner, planes, a * ck, b * ck) for a, b in spans]
    for message in z_out:
        message.arrive()
    ends = jnp.concatenate([dzr[0], dzr[1]], axis=0)
    end_hi, end_lo = split(ends)
    ends = jnp.concatenate([end_hi, end_lo], axis=0)
    for part, (a, b) in zip(halo, spans):
        part = part + tn(ends[:, inner:], pick[:, a * ck : b * ck])
        for c in range(a, b):
            piece = part[:, (c - a) * ck : (c - a + 1) * ck]
            dxs[1, c] = piece[0:cj]
            dxs[0, c] = piece[cj : 2 * cj]
            dys[1, c] = piece[y_row : y_row + ci]
            dys[0, c] = piece[y_row + ci : y_row + 2 * ci]
            for n in range(4):
                dxys[3 - n, c : c + 1] = piece[xy_row + n : xy_row + n + 1]
    for message in x_out + xy_out:
        message.start()

    for a, b in spans:
        part = spread(0, inner, a * ck, b * ck) + tn(ends[:, :inner], pick[:, a * ck : b * ck])
        for c in range(a, b):
            dep[c] = part[:, (c - a) * ck : (c - a + 1) * ck].reshape(ci, cj, ck)

    for message in x_out + xy_out:
        message.arrive()
    for s in range(2):
        plane = 0 if s == 0 else ci - 1
        dep[:, plane] += dxr[s]
    for s in range(2):
        row = 0 if s == 0 else cj - 1
        dep[:, :, row, :] += dyr[s]
        for t in range(2):
            plane = 0 if t == 0 else ci - 1
            dep[:, plane, row, :] += dxyr[t * 2 + s, 0:5]
    for message in x_in + y_in + z_in + z_out + x_out + xy_out:
        message.leave()


def local(counts, vel, sca, pos, mot, heat, size, li, lj, lk, tally):
    ci, cj, ck = vel.shape[1:]
    slots = heat.shape[0]
    outer = 2 * cj + 2 * ci + 4
    planes = ci * cj + -(-outer // 128) * 128
    vmem = pl.BlockSpec(memory_space=pltpu.VMEM)
    row = lambda value: value.reshape(1, slots)
    messages = 24
    scratch = [
        pltpu.VMEM((6, ci, cj, ck), F32),
        pltpu.VMEM((6 * ck, planes), BF16),
        pltpu.VMEM((6 * ck, planes), BF16),
        pltpu.VMEM((planes, slots), BF16),
        pltpu.VMEM((planes, slots), BF16),
        pltpu.VMEM((ck, slots), F32),
        pltpu.VMEM((5 * ck, slots), BF16),
        pltpu.VMEM((5 * ck, slots), BF16),
        pltpu.VMEM((8, slots), F32),
        pltpu.VMEM((2, 6, cj, ck), F32),
        pltpu.VMEM((2, 6, ci, ck), F32),
        pltpu.VMEM((4, 8, ck), F32),
        pltpu.VMEM((2, 8, planes), F32),
        pltpu.VMEM((2, 6, ci, ck), F32),
        pltpu.VMEM((4, 8, ck), F32),
        pltpu.VMEM((2, 8, planes), F32),
        pltpu.VMEM((2, 5, cj, ck), F32),
        pltpu.VMEM((2, 5, ci, ck), F32),
        pltpu.VMEM((4, 8, ck), F32),
        pltpu.VMEM((2, 8, planes), F32),
        pltpu.VMEM((2, 5, cj, ck), F32),
        pltpu.VMEM((2, 5, ci, ck), F32),
        pltpu.VMEM((4, 8, ck), F32),
        pltpu.VMEM((2, 8, planes), F32),
        pltpu.SemaphoreType.DMA((2,)),
        pltpu.SemaphoreType.DMA((messages,)),
        pltpu.SemaphoreType.DMA((messages,)),
    ]
    return pl.pallas_call(
        functools.partial(kernel, counts),
        out_shape=(
            jax.ShapeDtypeStruct((5, ci, cj, ck), F32),
            jax.ShapeDtypeStruct((5, slots), F32),
        ),
        in_specs=[pl.BlockSpec(memory_space=pl.ANY)] * 2
        + [vmem] * 7
        + [pl.BlockSpec(memory_space=pltpu.SMEM)],
        out_specs=(vmem, vmem),
        scratch_shapes=scratch,
        compiler_params=pltpu.CompilerParams(collective_id=0, has_side_effects=True),
    )(vel, sca, pos, mot, row(heat), row(size), row(li), row(lj), row(lk), tally)


def solution(mesh):
    bricks = P(None, AXES[0], AXES[1], AXES[2])
    rows = P(None, AXES)
    flat = P(AXES)
    counts = tuple(mesh.shape[axis] for axis in AXES)
    return jax.shard_map(
        functools.partial(local, counts),
        mesh=mesh,
        in_specs=(bricks, bricks, rows, rows) + (flat,) * 6,
        out_specs=(bricks, rows),
        check_vma=False,
    )
```

profile of v0, /device:TPU:0, one launch (start us, length us, event | category | flops | bytes accessed | tf_op | source)
XLA Modules:
  0.0 31.1 jit_solution(15886225970248765965)
XLA Ops:
  1.3 26.7 %shard_map.113 = (f32[5,8,64,128]{3,2,1,0:T(8,128)}, f32[5,1024]{1,0:T(8,128)}) custom-call(f32[3,8,64,128]{3,2,1,0:T(8,128)} %vel.1, f32[3,8,64,128]{3,2,1,0:T(8,128)} %sca.1, f32[3,1024]{1,0:T(4,128)} %pos.1, f32[3,1024]{1,0:T(4,128)} %mot.1, f32[1,1024]{1,0:T(1,128)} %bitcast.5, f32[1,1024]{1,0:T(1,128)} %bitcast.6, s32[1,1024]{1,0:T(1,128)} %bitcast.7, ...), custom_call_target="tpu_custom_call" | custom-call | tf_op jit(solution)/shard_map/pallas_call | solution.py:427
  28.0 0.0 copy-start
  28.0 2.5 %copy.15 = f32[5,8,64,128]{3,2,1,0:T(8,128)} copy(f32[5,8,64,128]{3,2,1,0:T(8,128)} %get-tuple-element.4) | data formatting | bytes 2621440
  30.5 0.0 copy-done
  30.5 0.6 %copy.16 = f32[5,1024]{1,0:T(8,128)} copy(f32[5,1024]{1,0:T(8,128)S(1)} %copy-done) | data formatting | bytes 40960
Async XLA Ops:
  28.0 2.5 %copy-start = (f32[5,1024]{1,0:T(8,128)S(1)}, f32[5,1024]{1,0:T(8,128)}, u32[]{:S(2)}) copy-start(f32[5,1024]{1,0:T(8,128)} %get-tuple-element.5) | copy-start | bytes 61444
where the time goes:
time: 31.7 us; the launch traced here: 31.1 us
  Pallas kernels  26.7 us (84%)
  local copies, waits for them, and re-layouts  3.15 us (10%)
  between operations  1.3 us (4%)
    pallas_call x1, Pallas kernels, local(): pl.pallas_call(functools.partial(kernel, counts), out_shape=(jax.ShapeDty...  26.7 us
    unnamed x4, local copies, waits for them, and re-layouts  3.15 us

commit v1 on v0

--- a/solution.py
+++ b/solution.py
@@ -52,16 +52,19 @@
     counts,
     vel,
     sca,
-    pos,
-    mot,
-    heat,
-    size,
-    li,
-    lj,
-    lk,
+    pos_hbm,
+    mot_hbm,
+    heat_hbm,
+    size_hbm,
+    li_hbm,
+    lj_hbm,
+    lk_hbm,
     tally,
     dep,
     state,
+    dxr,
+    dyr,
+    dxyr,
     fields,
     ft_hi,
     ft_lo,
@@ -82,10 +85,14 @@
     dys,
     dxys,
     dzs,
-    dxr,
-    dyr,
-    dxyr,
     dzr,
+    pos,
+    mot,
+    heat,
+    size,
+    li,
+    lj,
+    lk,
     load_sem,
     send_sem,
     recv_sem,
@@ -188,6 +195,17 @@
         pltpu.make_async_copy(vel, fields.at[0:3], load_sem.at[0]),
         pltpu.make_async_copy(sca, fields.at[3:6], load_sem.at[1]),
     ]
+    small = [
+        (pos_hbm, pos),
+        (mot_hbm, mot),
+        (heat_hbm, heat),
+        (size_hbm, size),
+        (li_hbm, li),
+        (lj_hbm, lj),
+        (lk_hbm, lk),
+    ]
+    for n, (src, dst) in enumerate(small):
+        loads.append(pltpu.make_async_copy(src, dst, load_sem.at[2 + n]))
     for load in loads:
         load.start()
     for message in x_in + y_in + z_in + z_out + x_out + xy_out:
@@ -374,17 +392,32 @@
 
     for message in x_out + xy_out:
         message.arrive()
-    for s in range(2):
-        plane = 0 if s == 0 else ci - 1
-        dep[:, plane] += dxr[s]
-    for s in range(2):
-        row = 0 if s == 0 else cj - 1
-        dep[:, :, row, :] += dyr[s]
-        for t in range(2):
-            plane = 0 if t == 0 else ci - 1
-            dep[:, plane, row, :] += dxyr[t * 2 + s, 0:5]
     for message in x_in + y_in + z_in + z_out + x_out + xy_out:
         message.leave()
+
+
+def finish(part, old, dxr, dyr, dxyr, dep_hbm, state_hbm, dep, sem):
+    ci, cj = dep.shape[1:3]
+    side = pltpu.make_async_copy(old, state_hbm, sem.at[0])
+    side.start()
+    outs = []
+    for c in range(5):
+        dep[c] = part[c]
+        for s in range(2):
+            plane = 0 if s == 0 else ci - 1
+            dep[c, plane] += dxr[s, c]
+        for s in range(2):
+            row = 0 if s == 0 else cj - 1
+            dep[c, :, row, :] += dyr[s, c]
+            for t in range(2):
+                plane = 0 if t == 0 else ci - 1
+                dep[c, plane, row : row + 1, :] += dxyr[t * 2 + s, c : c + 1]
+        out = pltpu.make_async_copy(dep.at[c], dep_hbm.at[c], sem.at[1 + c])
+        out.start()
+        outs.append(out)
+    for out in outs:
+        out.wait()
+    side.wait()
 
 
 def local(counts, vel, sca, pos, mot, heat, size, li, lj, lk, tally):
@@ -416,27 +449,48 @@
         pltpu.VMEM((2, 5, ci, ck), F32),
         pltpu.VMEM((4, 8, ck), F32),
         pltpu.VMEM((2, 8, planes), F32),
-        pltpu.VMEM((2, 5, cj, ck), F32),
-        pltpu.VMEM((2, 5, ci, ck), F32),
-        pltpu.VMEM((4, 8, ck), F32),
         pltpu.VMEM((2, 8, planes), F32),
-        pltpu.SemaphoreType.DMA((2,)),
+        pltpu.VMEM((3, slots), F32),
+        pltpu.VMEM((3, slots), F32),
+        pltpu.VMEM((1, slots), F32),
+        pltpu.VMEM((1, slots), F32),
+        pltpu.VMEM((1, slots), jnp.int32),
+        pltpu.VMEM((1, slots), jnp.int32),
+        pltpu.VMEM((1, slots), jnp.int32),
+        pltpu.SemaphoreType.DMA((9,)),
         pltpu.SemaphoreType.DMA((messages,)),
         pltpu.SemaphoreType.DMA((messages,)),
     ]
-    return pl.pallas_call(
+    any_ = pl.BlockSpec(memory_space=pl.ANY)
+    pin = lambda value: pltpu.with_memory_space_constraint(value, pltpu.HBM)
+    arrays = (vel, sca, pos, mot, row(heat), row(size), row(li), row(lj), row(lk))
+    part, state, dxr, dyr, dxyr = pl.pallas_call(
         functools.partial(kernel, counts),
         out_shape=(
             jax.ShapeDtypeStruct((5, ci, cj, ck), F32),
             jax.ShapeDtypeStruct((5, slots), F32),
+            jax.ShapeDtypeStruct((2, 5, cj, ck), F32),
+            jax.ShapeDtypeStruct((2, 5, ci, ck), F32),
+            jax.ShapeDtypeStruct((4, 8, ck), F32),
         ),
-        in_specs=[pl.BlockSpec(memory_space=pl.ANY)] * 2
-        + [vmem] * 7
-        + [pl.BlockSpec(memory_space=pltpu.SMEM)],
-        out_specs=(vmem, vmem),
+        in_specs=[pl.BlockSpec(memory_space=pltpu.HBM)] * 9 + [pl.BlockSpec(memory_space=pltpu.SMEM)],
+        out_specs=(vmem,) * 5,
         scratch_shapes=scratch,
-        compiler_params=pltpu.CompilerParams(collective_id=0, has_side_effects=True),
-    )(vel, sca, pos, mot, row(heat), row(size), row(li), row(lj), row(lk), tally)
+        compiler_params=pltpu.CompilerParams(
+            collective_id=0, has_side_effects=True, vmem_limit_bytes=24 * 2**20
+        ),
+    )(*[pin(x) for x in arrays], tally)
+    return pl.pallas_call(
+        finish,
+        out_shape=(
+            jax.ShapeDtypeStruct((5, ci, cj, ck), F32),
+            jax.ShapeDtypeStruct((5, slots), F32),
+        ),
+        in_specs=[vmem] * 5,
+        out_specs=(any_, any_),
+        scratch_shapes=[pltpu.VMEM((5, ci, cj, ck), F32), pltpu.SemaphoreType.DMA((6,))],
+        compiler_params=pltpu.CompilerParams(vmem_limit_bytes=12 * 2**20),
+    )(part, state, dxr, dyr, dxyr)
 
 
 def solution(mesh):

time: 31.7 us -> 27.7 us (0.87)
  local copies, waits for them, and re-layouts: 3.15 us -> 0 us
  Pallas kernels: 26.7 us -> 26 us
    unnamed x4 -> x0, local copies, waits for them, and re-layouts: 3.15 us -> none
    pallas_call x1, Pallas kernels: 26.7 us -> 24.9 us  [local(): pl.pallas_call(functools.partial(kernel, counts), out_shape=(jax.ShapeDty...]
    pallas_call x0 -> x1, Pallas kernels: none -> 1.15 us  [local(): pl.pallas_call(finish, out_shape=(jax.ShapeDtypeStruct((5, ci, cj, ck), F...]
where the time goes in v1:
time: 27.7 us; the launch traced here: 27.3 us
  Pallas kernels  26 us (94%)
  between operations  1.29 us (5%)
    pallas_call x1, Pallas kernels, local(): pl.pallas_call(functools.partial(kernel, counts), out_shape=(jax.ShapeDty...  24.9 us
    pallas_call x1, Pallas kernels, local(): pl.pallas_call(finish, out_shape=(jax.ShapeDtypeStruct((5, ci, cj, ck), F...  1.15 us

profile of v1, /device:TPU:0, one launch (start us, length us, event | category | flops | bytes accessed | tf_op | source)
XLA Modules:
  0.0 27.3 jit_solution(4487938548424154667)
XLA Ops:
  1.3 24.9 %shard_map.113 = (f32[5,8,64,128]{3,2,1,0:T(8,128)S(1)}, f32[5,1024]{1,0:T(8,128)S(1)}, f32[2,5,64,128]{3,2,1,0:T(8,128)S(1)}, f32[2,5,8,128]{3,2,1,0:T(8,128)S(1)}, f32[4,8,128]{2,1,0:T(8,128)S(1)}) custom-call(f32[3,8,64,128]{3,2,1,0:T(8,128)} %vel.1, f32[3,8,64,128]{3,2,1,0:T(8,128)} %sca.1, f32[3,1024]{1,0:T(4,128)} %pos_hbm.1, f32[3,1024]{1,0:T(4,128)} %mot_hbm.1, ...), custom_call_target="tpu_custom_call" | custom-call | tf_op jit(solution)/shard_map/pallas_call | solution.py:467
  26.1 1.2 %shard_map.114 = (f32[5,8,64,128]{3,2,1,0:T(8,128)}, f32[5,1024]{1,0:T(8,128)}) custom-call(f32[5,8,64,128]{3,2,1,0:T(8,128)S(1)} %get-tuple-element.7.part, f32[5,1024]{1,0:T(8,128)S(1)} %get-tuple-element.8.old, f32[2,5,64,128]{3,2,1,0:T(8,128)S(1)} %get-tuple-element.9.dxr, f32[2,5,8,128]{3,2,1,0:T(8,128)S(1)} %get-tuple-element.10.dyr, ...), custom_call_target="tpu_custom_call" | custom-call | tf_op jit(solution)/shard_map/pallas_call | solution.py:483

commit v2 on v0

v2 whole, which is shorter than its diff:
```python
import functools

import jax
import jax.numpy as jnp
from jax import lax
from jax.experimental import pallas as pl
from jax.experimental.pallas import tpu as pltpu
from jax.sharding import PartitionSpec as P

TILE = 128
AXES = ("gx", "gy", "gz")
MESH = pl.DeviceIdType.MESH
F32 = jnp.float32
BF16 = jnp.bfloat16

step_time = 0.25
evap_rate = 1.0
heat_rate = 2.0
boiling_energy_drain = 0.3

STEPS = ((1, 0), (-1, 1))
NUM_TERMS = 5
NUM_FIELDS = 6


def split(value):
    high = value.astype(BF16)
    return high, (value - high.astype(F32)).astype(BF16)


def nn(a, b):
    return lax.dot_general(a, b, (((1,), (0,)), ((), ())), preferred_element_type=F32)


def nt(a, b):
    return lax.dot_general(a, b, (((1,), (1,)), ((), ())), preferred_element_type=F32)


def pair_weights(offset):
    lower = jnp.where(offset < 0.0, -1.0, 0.0)
    first = jnp.maximum(0.0, 1.0 - jnp.abs(offset - lower))
    second = jnp.maximum(0.0, 1.0 - jnp.abs(offset - (lower + 1.0)))
    return first, second, lower


def lanes_of(shape):
    return lax.broadcasted_iota(jnp.int32, shape, len(shape) - 1)


def spots(first, count, base, wa, wb):
    rows = (lax.broadcasted_iota(jnp.int32, (count, base.shape[1]), 0) + first).astype(F32)
    return jnp.where(rows == base, wa, jnp.where(rows == base + 1.0, wb, 0.0))


def kernel(
    counts,
    vel,
    sca,
    pos_in,
    mot_in,
    heat_in,
    size_in,
    li_in,
    lj_in,
    lk_in,
    tally,
    dep,
    state,
    dyr,
    dxyr,
    dzr,
    dxzr,
    dyzr,
    dxyzr,
    fields,
    pos,
    mot,
    heat,
    size,
    li,
    lj,
    lk,
    ft_hi,
    ft_lo,
    w_hi,
    w_lo,
    wx,
    wy,
    xt,
    yt_hi,
    yt_lo,
    line,
    line_hi,
    line_lo,
    ztable,
    src_hi,
    src_lo,
    sampled,
    geo,
    terms,
    xh,
    yh,
    xyh,
    zh,
    xzh,
    yzh,
    xyzh,
    geor,
    termr,
    ys,
    xys,
    zs,
    ez,
    dys,
    dxys,
    dzs,
    dxzs,
    dyzs,
    load_sem,
    send_sem,
    recv_sem,
):
    ci, cj, ck = vel.shape[1:]
    slots = heat.shape[1]
    inner = ci * cj
    me = [lax.axis_index(axis) for axis in AXES]

    def exists(move, sign):
        good = None
        for d in range(3):
            step = sign * move[d]
            if step == 1:
                test = me[d] < counts[d] - 1
            elif step == -1:
                test = me[d] > 0
            else:
                continue
            good = test if good is None else jnp.logical_and(good, test)
        return good

    def peer(move):
        return tuple(lax.rem(me[d] + move[d] + counts[d], counts[d]) for d in range(3))

    class Message:
        def __init__(self, number, move, src, dst):
            self.move = move
            self.dst = dst
            self.copy = pltpu.make_async_remote_copy(
                src_ref=src,
                dst_ref=dst,
                send_sem=send_sem.at[number],
                recv_sem=recv_sem.at[number],
                device_id=peer(move),
                device_id_type=MESH,
            )

        def start(self):
            @pl.when(exists(self.move, 1))
            def _():
                self.copy.start()

        def blank(self):
            @pl.when(jnp.logical_not(exists(self.move, -1)))
            def _():
                self.dst[...] = jnp.zeros(self.dst.shape, F32)

        def arrive(self):
            @pl.when(exists(self.move, -1))
            def _():
                self.copy.wait_recv()

        def leave(self):
            @pl.when(exists(self.move, 1))
            def _():
                self.copy.wait_send()

    made = []

    def add(group, move, src, dst):
        message = Message(len(made), move, src, dst)
        made.append(message)
        group.append(message)

    face = lambda n, extent: extent - 1 if n == 0 else 0
    edge_tile = lambda n: pl.ds(face(n, ci) * cj // 128 * 128, 128)
    moves = []
    x_in, y_in, z_in, geo_in, x_out, y_out, z_out = [], [], [], [], [], [], []
    for mx, x in STEPS:
        add(x_in, (mx, 0, 0), fields.at[:, face(x, ci)], xh.at[x])
        add(geo_in, (mx, 0, 0), geo, geor.at[x])
        add(x_out, (mx, 0, 0), terms, termr.at[x])
        moves.append((mx, 0, 0))
        for my, y in STEPS:
            add(y_in, (mx, my, 0), xys.at[2 * x + y], xyh.at[2 * x + y])
            add(y_out, (mx, my, 0), dxys.at[2 * x + y], dxyr.at[2 * x + y])
            moves.append((mx, my, 0))
            for mz, z in STEPS:
                n = 4 * x + 2 * y + z
                add(z_in, (mx, my, mz), ez.at[z], xyzh.at[n])
                add(z_out, (mx, my, mz), dxzs.at[2 * x + z], dxyzr.at[n])
                moves.append((mx, my, mz))
        for mz, z in STEPS:
            n = 2 * x + z
            add(z_in, (mx, 0, mz), zs.at[z, :, edge_tile(x)], xzh.at[n])
            add(z_out, (mx, 0, mz), dxzs.at[n], dxzr.at[n])
            moves.append((mx, 0, mz))
    for my, y in STEPS:
        add(y_in, (0, my, 0), ys.at[y], yh.at[y])
        add(y_out, (0, my, 0), dys.at[y, :, 0:ci], dyr.at[y])
        moves.append((0, my, 0))
        for mz, z in STEPS:
            add(z_in, (0, my, mz), ez.at[z], yzh.at[2 * y + z])
            add(z_out, (0, my, mz), dyzs.at[z], dyzr.at[2 * y + z])
            moves.append((0, my, mz))
    for mz, z in STEPS:
        add(z_in, (0, 0, mz), zs.at[z], zh.at[z])
        add(z_out, (0, 0, mz), dzs.at[z, :, 0:ci], dzr.at[z])
        moves.append((0, 0, mz))

    barrier = pltpu.get_barrier_semaphore()
    for move in moves:

        @pl.when(exists(move, 1))
        def _():
            pl.semaphore_signal(barrier, inc=1, device_id=peer(move), device_id_type=MESH)

    small = [
        pltpu.make_async_copy(src, dst, load_sem.at[2 + n])
        for n, (src, dst) in enumerate(
            [
                (pos_in, pos),
                (li_in, li),
                (lj_in, lj),
                (lk_in, lk),
                (mot_in, mot),
                (heat_in, heat),
                (size_in, size),
            ]
        )
    ]
    loads = [
        pltpu.make_async_copy(vel, fields.at[0:3], load_sem.at[0]),
        pltpu.make_async_copy(sca, fields.at[3:6], load_sem.at[1]),
    ]
    for load in small + loads:
        load.start()
    for message in y_in + z_in + y_out + z_out:
        message.blank()
    zs[...] = jnp.zeros_like(zs)
    xys[...] = jnp.zeros_like(xys)
    dxys[...] = jnp.zeros_like(dxys)
    dxzs[...] = jnp.zeros_like(dxzs)

    for load in small:
        load.wait()
    xa, xb, lx = pair_weights(pos[0:1])
    ya, yb, ly = pair_weights(pos[1:2])
    za, zb, lz = pair_weights(pos[2:3])
    i0 = li[...].astype(F32) + lx
    j0 = lj[...].astype(F32) + ly
    k0 = lk[...].astype(F32) + lz

    def at(index, base, wa, wb):
        return jnp.where(base == index, wa, jnp.where(base + 1.0 == index, wb, 0.0))

    x_low, x_high = at(-1.0, i0, xa, xb), at(float(ci), i0, xa, xb)
    y_low, y_high = at(-1.0, j0, ya, yb), at(float(cj), j0, ya, yb)
    z_low, z_high = at(-1.0, k0, za, zb), at(float(ck), k0, za, zb)
    for n, row in enumerate((x_high, x_low, j0, k0, ya, yb, za, zb)):
        geo[n : n + 1] = row
    xt[0:ci] = spots(0, ci, i0, xa, xb)
    xt[ci : 2 * ci] = jnp.concatenate([x_low, x_high, jnp.zeros((ci - 2, slots), F32)], axis=0)
    across = spots(0, cj, j0, ya, yb)
    rims = [
        jnp.broadcast_to(y_low, (8, slots)),
        jnp.broadcast_to(y_high, (8, slots)),
        jnp.zeros((yt_hi.shape[0] - cj - 16, slots), F32),
    ]
    yt_hi[...], yt_lo[...] = split(jnp.concatenate([across] + rims, axis=0))
    for i in range(ci):
        high, low = split(xt[i : i + 1] * across)
        w_hi[i * cj : (i + 1) * cj] = high
        w_lo[i * cj : (i + 1) * cj] = low
    for n, row in enumerate((x_low, x_high)):
        high, low = split(row * across)
        wx[n, 0:cj] = high
        wx[n, cj : 2 * cj] = high
        wx[n, 2 * cj : 3 * cj] = low
    corners = [a * b for a in (x_low, x_high) for b in (y_low, y_high)]
    sides = [xt[0:ci] * y_low, xt[0:ci] * y_high]
    group = wy.shape[0] // 4
    filler = [jnp.zeros((group - 2 * ci - 4, slots), F32)]
    high, low = split(jnp.concatenate(sides + corners + filler, axis=0))
    wy[0:group] = high
    wy[group : 2 * group] = high
    wy[2 * group : 3 * group] = low
    wy[3 * group : 4 * group] = jnp.zeros((group, slots), BF16)
    line[...] = spots(0, ck, k0, za, zb)
    line_hi[...], line_lo[...] = split(line[...])

    for load in loads:
        load.wait()
    for y in range(2):
        row = face(y, cj)
        ys[y] = fields[:, :, row, :]
        for x in range(2):
            xys[2 * x + y, 0:NUM_FIELDS] = fields[:, face(x, ci), row, :]
    pl.semaphore_wait(barrier, sum(exists(move, 1).astype(jnp.int32) for move in moves))

    for message in x_in + y_in + geo_in:
        message.start()

    for f in range(NUM_FIELDS):
        turned = fields[f].reshape(inner, ck).T
        high, low = split(turned)
        ft_hi[f * ck : (f + 1) * ck] = high
        ft_lo[f * ck : (f + 1) * ck] = low
        zs[0, f : f + 1] = turned[ck - 1 : ck]
        zs[1, f : f + 1] = turned[0:1]
    rows = lax.broadcasted_iota(jnp.int32, (inner, 128), 0)
    cols = lanes_of((inner, 128))
    target = jnp.where(cols < cj + 8, (cols - cj) * cj + cj - 1, (cols - cj - 8) * cj)
    chosen = (rows == target) & (cols >= cj) & (cols < cj + 16)
    chosen = jnp.where(chosen, 1.0, 0.0).astype(BF16)
    high, low = split(zs[...].reshape(16, inner))
    ez[...] = (nn(high, chosen) + nn(low, chosen)).reshape(2, 8, 128)
    for message in z_in:
        message.start()

    width = 256

    def collect(got, here):
        return [
            jnp.sum(got[f * ck : (f + 1) * ck] * line[:, here], axis=0, keepdims=True)
            for f in range(NUM_FIELDS)
        ]

    for s in range(0, slots, width):
        here = slice(s, s + width)
        got = nn(ft_hi[...], w_hi[:, here])
        got += nn(ft_hi[...], w_lo[:, here])
        got += nn(ft_lo[...], w_hi[:, here])
        for f, part in enumerate(collect(got, here)):
            sampled[f : f + 1, here] = part

    for message in y_in:
        message.arrive()

    def turn(flats):
        out = []
        for flat in flats:
            high = flat.astype(BF16).astype(F32)
            out.append(jnp.concatenate([high, flat - high, high], axis=0).T.astype(BF16))
        return jnp.concatenate(out, axis=0)

    def more(left, right):
        for s in range(0, slots, width):
            here = slice(s, s + width)
            for f, part in enumerate(collect(nn(left, right[:, here]), here)):
                sampled[f : f + 1, here] += part

    empty = jnp.zeros((group - 2 * ci - 4, ck), F32)
    left = turn(
        [
            jnp.concatenate(
                [yh[0, f], yh[1, f]] + [xyh[q, f : f + 1] for q in range(4)] + [empty], axis=0
            )
            for f in range(NUM_FIELDS)
        ]
    )
    more(left, wy[0 : 3 * group])

    for message in z_in:
        message.arrive()
    lanes = lanes_of((8, 128))
    body = lanes < cj

    def half(tile, odd):
        return jnp.where(body, pltpu.roll(tile, 128 - cj, 1) if odd else tile, 0.0)

    def pick(tile, lane):
        return jnp.where(lanes == lane, tile, 0.0)

    for z in range(2):
        for i in range(ci):
            first = i * cj // 128 * 128
            block = half(zh[z, :, first : first + 128], i * cj % 128 != 0)
            block += pick(yzh[z], cj + i) + pick(yzh[2 + z], cj + 8 + i)
            ztable[z, i] = block
        for x in range(2):
            i = face(x, ci)
            block = half(xzh[2 * x + z], i * cj % 128 != 0)
            block += pick(xyzh[4 * x + z], cj + i) + pick(xyzh[4 * x + 2 + z], cj + 8 + i)
            ztable[z, ci + x] = block
    blocks = ci + 2
    high, low = split(ztable[...].reshape(2 * blocks * 8, 128))
    got = nn(high, yt_hi[...]) + nn(high, yt_lo[...]) + nn(low, yt_hi[...])
    for z, rim in enumerate((z_low, z_high)):
        total = None
        for b in range(blocks):
            first = (z * blocks + b) * 8
            part = got[first : first + 8] * xt[b : b + 1]
            total = part if total is None else total + part
        sampled[...] += total * rim

    for x, message in enumerate(x_in):

        @pl.when(exists(message.move, -1))
        def _():
            message.copy.wait_recv()
            more(turn([xh[x, f] for f in range(NUM_FIELDS)]), wx[x])

    gas = sampled[...]
    live = lanes_of((1, slots)) // TILE < tally[0]
    q = size[...]
    tp = heat[...]
    v = mot[...]
    drag = step_time / (0.5 * q)
    v_new = (v + drag * gas[0:3]) / (1.0 + drag)
    mass = q * jnp.sqrt(q)
    share = jnp.exp(4.0 * (tp - 1.0))
    decay = step_time * evap_rate * gas[5:6] * (share - gas[4:5])
    q_new = q - decay
    mass_new = q_new * jnp.sqrt(q_new)
    conduct = step_time * heat_rate * gas[5:6] / q
    tp_new = (tp + conduct * gas[3:4]) / (1.0 + conduct) - boiling_energy_drain * decay / q
    state[0:3] = jnp.where(live, v_new, v)
    state[3:4] = jnp.where(live, tp_new, tp)
    state[4:5] = jnp.where(live, q_new, q)
    terms[0:3] = jnp.where(live, mass * (v - v_new), 0.0)
    terms[3:4] = jnp.where(live, mass * (tp - tp_new), 0.0)
    terms[4:5] = jnp.where(live, mass - mass_new, 0.0)
    for message in x_out:
        message.start()

    part_rows = 2 * ci
    pieces = [xt[...] * terms[c : c + 1] for c in range(NUM_TERMS)]

    def fan(rims):
        return split(jnp.concatenate([piece * rim for rim in rims for piece in pieces], axis=0))

    def both(high, low, right_hi, right_lo):
        return nt(high, right_hi) + nt(high, right_lo) + nt(low, right_hi)

    shape = (2, NUM_TERMS, part_rows, 128)
    high, low = fan((y_high, y_low))
    dys[...] = both(high, low, line_hi[...], line_lo[...]).reshape(shape)
    for x in range(2):
        row = ci + 1 - x
        for y in range(2):
            for c in range(NUM_TERMS):
                dxys[2 * x + y, c : c + 1] = dys[y, c, row : row + 1]
    for message in y_out:
        message.start()
    high, low = fan((z_high, z_low))
    dzs[...] = both(high, low, yt_hi[...], yt_lo[...]).reshape(shape)
    for z in range(2):
        for x in range(2):
            row = ci + 1 - x
            for c in range(NUM_TERMS):
                dxzs[2 * x + z, c : c + 1] = dzs[z, c, row : row + 1]
        tile = jnp.zeros((8, 128), F32)
        for c in range(NUM_TERMS):
            keep = (lanes == cj + c) | (lanes == cj + 8 + c)
            tile = jnp.where(keep, dzs[z, c, 0:ci], tile)
        dyzs[z] = tile
    for message in z_out:
        message.start()

    for c in range(NUM_TERMS):
        high, low = split(line[...] * terms[c : c + 1])
        src_hi[c * ck : (c + 1) * ck] = high
        src_lo[c * ck : (c + 1) * ck] = low
    for a in range(0, NUM_TERMS, 2):
        b = min(a + 2, NUM_TERMS)
        span = slice(a * ck, b * ck)
        got = nt(w_hi[...], src_hi[span])
        got += nt(w_hi[...], src_lo[span])
        got += nt(w_lo[...], src_hi[span])
        for c in range(a, b):
            dep[c] = got[:, (c - a) * ck : (c - a + 1) * ck].reshape(ci, cj, ck)

    for x, (places, deposits) in enumerate(zip(geo_in, x_out)):
        plane = 0 if x == 0 else ci - 1

        @pl.when(exists(places.move, -1))
        def _():
            places.copy.wait_recv()
            rows = [geor[x, n : n + 1] for n in range(8)]
            there = spots(0, cj, rows[2], rows[4], rows[5]) * rows[x]
            along_hi, along_lo = split(spots(0, ck, rows[3], rows[6], rows[7]))
            deposits.copy.wait_recv()
            high, low = split(
                jnp.concatenate([there * termr[x, c : c + 1] for c in range(NUM_TERMS)], axis=0)
            )
            got = both(high, low, along_hi, along_lo)
            for c in range(NUM_TERMS):
                dep[c, plane] += got[c * cj : (c + 1) * cj]

    for message in y_out + z_out:
        message.arrive()
    for message in made:
        message.leave()


def finish(
    part, old, dyr, dxyr, dzr, dxzr, dyzr, dxyzr, dep_out, state_out, dep, sem
):
    ci, cj, ck = dep.shape[1:]
    terms = dep.shape[0]
    side = pltpu.make_async_copy(old, state_out, sem.at[terms])
    side.start()
    lanes = lanes_of((8, 128))
    rows = lax.broadcasted_iota(jnp.int32, (8, 128), 0)
    ends = (0, ck - 1)

    def at_ends(first, second, where):
        return jnp.where(where == ends[0], first, jnp.where(where == ends[1], second, 0.0))

    corner = []
    for x in range(2):
        for y in range(2):
            lane = cj + 8 if y == 0 else cj
            first, second = (dxyzr[4 * x + 2 * y + z, :, lane : lane + 1] for z in range(2))
            corner.append(dxyr[2 * x + y] + at_ends(first, second, lanes))
    wide = lanes_of((cj, ck))
    outs = []
    for c in range(terms):
        turned = []
        for z in range(2):
            block = dzr[z, c]
            for x in range(2):
                plane = 0 if x == 0 else ci - 1
                block += jnp.where(rows == plane, dxzr[2 * x + z, c : c + 1], 0.0)
            turned.append(block)
        turned = jnp.concatenate(turned, axis=0).T
        for i in range(ci):
            first, second = turned[0:cj, i : i + 1], turned[0:cj, ci + i : ci + i + 1]
            dep[c, i] = part[c, i] + at_ends(first, second, wide)
        for y in range(2):
            row = 0 if y == 0 else cj - 1
            lane = cj + 8 + c if y == 0 else cj + c
            first, second = (dyzr[2 * y + z, :, lane : lane + 1] for z in range(2))
            dep[c, :, row, :] += dyr[y, c] + at_ends(first, second, lanes)
            for x in range(2):
                plane = 0 if x == 0 else ci - 1
                dep[c, plane, row : row + 1, :] += corner[2 * x + y][c : c + 1]
        out = pltpu.make_async_copy(dep.at[c], dep_out.at[c], sem.at[c])
        out.start()
        outs.append(out)
    for out in outs:
        out.wait()
    side.wait()


def local(counts, vel, sca, pos, mot, heat, size, li, lj, lk, tally):
    ci, cj, ck = vel.shape[1:]
    slots = heat.shape[0]
    inner = ci * cj
    vmem = pl.BlockSpec(memory_space=pltpu.VMEM)
    hbm = pl.BlockSpec(memory_space=pltpu.HBM)
    row = lambda value: value.reshape(1, slots)
    pin = lambda value: pltpu.with_memory_space_constraint(value, pltpu.HBM)
    tile = (8, 128)
    group = -(-(2 * ci + 4) // 16) * 16
    messages = 54
    f32 = lambda *shape: pltpu.VMEM(shape, F32)
    i32 = lambda *shape: pltpu.VMEM(shape, jnp.int32)
    b16 = lambda *shape: pltpu.VMEM(shape, BF16)
    struct = lambda *shape: jax.ShapeDtypeStruct(shape, F32)
    scratch = [
        f32(NUM_FIELDS, ci, cj, ck),
        f32(3, slots),
        f32(3, slots),
        f32(1, slots),
        f32(1, slots),
        i32(1, slots),
        i32(1, slots),
        i32(1, slots),
        b16(NUM_FIELDS * ck, inner),
        b16(NUM_FIELDS * ck, inner),
        b16(inner, slots),
        b16(inner, slots),
        b16(2, 3 * cj, slots),
        b16(4 * group, slots),
        f32(2 * ci, slots),
        b16(128, slots),
        b16(128, slots),
        f32(ck, slots),
        b16(ck, slots),
        b16(ck, slots),
        f32(2, ci + 2, *tile),
        b16(NUM_TERMS * ck, slots),
        b16(NUM_TERMS * ck, slots),
        f32(8, slots),
        f32(8, slots),
        f32(NUM_TERMS, slots),
        f32(2, NUM_FIELDS, cj, ck),
        f32(2, NUM_FIELDS, ci, ck),
        f32(4, *tile),
        f32(2, 8, inner),
        f32(4, *tile),
        f32(4, *tile),
        f32(8, *tile),
        f32(2, 8, slots),
        f32(2, NUM_TERMS, slots),
        f32(2, NUM_FIELDS, ci, ck),
        f32(4, *tile),
        f32(2, 8, inner),
        f32(2, *tile),
        f32(2, NUM_TERMS, 2 * ci, ck),
        f32(4, *tile),
        f32(2, NUM_TERMS, 2 * ci, ck),
        f32(4, *tile),
        f32(2, *tile),
        pltpu.SemaphoreType.DMA((9,)),
        pltpu.SemaphoreType.DMA((messages,)),
        pltpu.SemaphoreType.DMA((messages,)),
    ]
    results = (
        struct(NUM_TERMS, ci, cj, ck),
        struct(NUM_TERMS, slots),
        struct(2, NUM_TERMS, ci, ck),
        struct(4, *tile),
        struct(2, NUM_TERMS, ci, ck),
        struct(4, *tile),
        struct(4, *tile),
        struct(8, *tile),
    )
    arrays = (vel, sca, pos, mot, row(heat), row(size), row(li), row(lj), row(lk))
    parts = pl.pallas_call(
        functools.partial(kernel, counts),
        out_shape=results,
        in_specs=[hbm] * len(arrays) + [pl.BlockSpec(memory_space=pltpu.SMEM)],
        out_specs=(vmem,) * len(results),
        scratch_shapes=scratch,
        compiler_params=pltpu.CompilerParams(
            collective_id=0, has_side_effects=True, vmem_limit_bytes=32 * 2**20
        ),
    )(*[pin(value) for value in arrays], tally)
    return pl.pallas_call(
        finish,
        out_shape=results[0:2],
        in_specs=[vmem] * len(results),
        out_specs=(pl.BlockSpec(memory_space=pl.ANY),) * 2,
        scratch_shapes=[
            f32(NUM_TERMS, ci, cj, ck),
            pltpu.SemaphoreType.DMA((NUM_TERMS + 1,)),
        ],
        compiler_params=pltpu.CompilerParams(vmem_limit_bytes=12 * 2**20),
    )(*parts)


def solution(mesh):
    bricks = P(None, AXES[0], AXES[1], AXES[2])
    rows = P(None, AXES)
    flat = P(AXES)
    counts = tuple(mesh.shape[axis] for axis in AXES)
    return jax.shard_map(
        functools.partial(local, counts),
        mesh=mesh,
        in_specs=(bricks, bricks, rows, rows) + (flat,) * 6,
        out_specs=(bricks, rows),
        check_vma=False,
    )
```

time: 31.7 us -> 23.6 us (0.74)
  Pallas kernels: 26.7 us -> 21.8 us
  local copies, waits for them, and re-layouts: 3.15 us -> 0 us
    pallas_call x1 -> x2, Pallas kernels: 26.7 us -> 21.8 us  [the longest x1 19.8 us: local(): pl.pallas_call(functools.partial(kernel, counts), out_shape=results, in_s...]
    unnamed x4 -> x0, local copies, waits for them, and re-layouts: 3.15 us -> none
where the time goes in v2:
time: 23.6 us; the launch traced here: 23.1 us
  Pallas kernels  21.8 us (92%)
  between operations  1.29 us (5%)
    pallas_call x1, Pallas kernels, local(): pl.pallas_call(functools.partial(kernel, counts), out_shape=results, in_s...  19.8 us
    pallas_call x1, Pallas kernels, local(): pl.pallas_call(finish, out_shape=results[0:2], in_specs=[vmem] * len(resu...  1.99 us

profile of v2, /device:TPU:0, one launch (start us, length us, event | category | flops | bytes accessed | tf_op | source)
XLA Modules:
  0.0 23.1 jit_solution(11525650753260787449)
XLA Ops:
  1.3 19.8 %shard_map.113 = (f32[5,8,64,128]{3,2,1,0:T(8,128)S(1)}, f32[5,1024]{1,0:T(8,128)S(1)}, f32[2,5,8,128]{3,2,1,0:T(8,128)S(1)}, f32[4,8,128]{2,1,0:T(8,128)S(1)}, ...) custom-call(f32[3,8,64,128]{3,2,1,0:T(8,128)} %vel.1, ...), custom_call_target="tpu_custom_call" | custom-call | tf_op jit(solution)/shard_map/pallas_call | solution.py:631
  21.1 2.0 %shard_map.114 = (f32[5,8,64,128]{3,2,1,0:T(8,128)}, f32[5,1024]{1,0:T(8,128)}) custom-call(f32[5,8,64,128]{3,2,1,0:T(8,128)S(1)} %get-tuple-element.10.part, f32[5,1024]{1,0:T(8,128)S(1)} %get-tuple-element.11.old, f32[2,5,8,128]{3,2,1,0:T(8,128)S(1)} %get-tuple-element.12.dyr, f32[4,8,128]{2,1,0:T(8,128)S(1)} %get-tuple-element.13.dxyr, ...), custom_call_target="tpu_custom_call" | custom-call | tf_op jit(solution)/shard_map/pallas_call | solution.py:641

commit v3 on v2

--- a/solution.py
+++ b/solution.py
@@ -1,4 +1,5 @@
 import functools
+import itertools
 
 import jax
 import jax.numpy as jnp
@@ -21,6 +22,8 @@
 STEPS = ((1, 0), (-1, 1))
 NUM_TERMS = 5
 NUM_FIELDS = 6
+PARTS = 3
+CHUNK = NUM_FIELDS // PARTS
 
 
 def split(value):
@@ -87,11 +90,10 @@
     wx,
     wy,
     xt,
-    yt_hi,
-    yt_lo,
+    cw,
+    yt,
     line,
-    line_hi,
-    line_lo,
+    lines,
     ztable,
     src_hi,
     src_lo,
@@ -116,6 +118,7 @@
     dzs,
     dxzs,
     dyzs,
+    gauge,
     load_sem,
     send_sem,
     recv_sem,
@@ -142,13 +145,15 @@
         return tuple(lax.rem(me[d] + move[d] + counts[d], counts[d]) for d in range(3))
 
     class Message:
-        def __init__(self, number, move, src, dst):
+        def __init__(self, number, move, src, dst, tiles, post):
             self.move = move
             self.dst = dst
+            self.tiles = tiles
+            self.number = number
             self.copy = pltpu.make_async_remote_copy(
                 src_ref=src,
                 dst_ref=dst,
-                send_sem=send_sem.at[number],
+                send_sem=send_sem.at[post],
                 recv_sem=recv_sem.at[number],
                 device_id=peer(move),
                 device_id_type=MESH,
@@ -164,58 +169,90 @@
             def _():
                 self.dst[...] = jnp.zeros(self.dst.shape, F32)
 
-        def arrive(self):
-            @pl.when(exists(self.move, -1))
-            def _():
-                self.copy.wait_recv()
-
         def leave(self):
             @pl.when(exists(self.move, 1))
             def _():
                 self.copy.wait_send()
 
+    def totals(messages, sign):
+        sides = []
+        for extent in counts:
+            low, high = (-1,), (1,)
+            sides.append([()] if extent == 1 else [low, high] + [low + high] * (extent > 2))
+        found = set()
+        for place in itertools.product(*sides):
+            there = [
+                message.tiles
+                for message in messages
+                if all(
+                    step == 0 or sign * step in side for step, side in zip(message.move, place)
+                )
+            ]
+            found.add(sum(there))
+        return sorted(found - {0})
+
+    def drain(sem, messages, sign):
+        count = sum(
+            jnp.where(exists(message.move, sign), message.tiles, 0) for message in messages
+        )
+        for total in totals(messages, sign):
+
+            @pl.when(count == total)
+            def _():
+                some = gauge.at[0:total]
+                pltpu.make_async_copy(some, some, sem).wait()
+
+    def arrive(messages):
+        drain(recv_sem.at[messages[0].number], messages, -1)
+
     made = []
 
-    def add(group, move, src, dst):
-        message = Message(len(made), move, src, dst)
+    def add(group, number, move, src, dst, tiles=1, post=0):
+        message = Message(number, move, src, dst, tiles, post)
         made.append(message)
         group.append(message)
 
+    Y_IN, Z_IN, OUT, GEO, TERMS, RIM, FACE = 0, 1, 2, 3, 5, 7, 9
     face = lambda n, extent: extent - 1 if n == 0 else 0
     edge_tile = lambda n: pl.ds(face(n, ci) * cj // 128 * 128, 128)
     moves = []
-    x_in, y_in, z_in, geo_in, x_out, y_out, z_out = [], [], [], [], [], [], []
+    y_in, z_in, geo_in, x_out, out = [], [], [], [], []
+    faces, rim_in = [[], []], [[], []]
     for mx, x in STEPS:
-        add(x_in, (mx, 0, 0), fields.at[:, face(x, ci)], xh.at[x])
-        add(geo_in, (mx, 0, 0), geo, geor.at[x])
-        add(x_out, (mx, 0, 0), terms, termr.at[x])
-        moves.append((mx, 0, 0))
         for my, y in STEPS:
-            add(y_in, (mx, my, 0), xys.at[2 * x + y], xyh.at[2 * x + y])
-            add(y_out, (mx, my, 0), dxys.at[2 * x + y], dxyr.at[2 * x + y])
-            moves.append((mx, my, 0))
+            add(y_in, Y_IN, (mx, my, 0), xys.at[2 * x + y], xyh.at[2 * x + y])
+            add(out, OUT, (mx, my, 0), dxys.at[2 * x + y], dxyr.at[2 * x + y])
             for mz, z in STEPS:
                 n = 4 * x + 2 * y + z
-                add(z_in, (mx, my, mz), ez.at[z], xyzh.at[n])
-                add(z_out, (mx, my, mz), dxzs.at[2 * x + z], dxyzr.at[n])
+                add(rim_in[x], RIM + x, (mx, my, mz), ez.at[z], xyzh.at[n])
+                add(out, OUT, (mx, my, mz), dxzs.at[2 * x + z], dxyzr.at[n])
                 moves.append((mx, my, mz))
+            moves.append((mx, my, 0))
+        for part in range(PARTS):
+            span = slice(part * CHUNK, (part + 1) * CHUNK)
+            here = fields.at[span, face(x, ci)]
+            add(faces[x], FACE + PARTS * x + part, (mx, 0, 0), here, xh.at[x, span], CHUNK * cj // 8)
+        add(geo_in, GEO + x, (mx, 0, 0), geo, geor.at[x], slots // 128)
+        add(x_out, TERMS + x, (mx, 0, 0), terms, termr.at[x], 0, 1 + x)
         for mz, z in STEPS:
             n = 2 * x + z
-            add(z_in, (mx, 0, mz), zs.at[z, :, edge_tile(x)], xzh.at[n])
-            add(z_out, (mx, 0, mz), dxzs.at[n], dxzr.at[n])
+            add(rim_in[x], RIM + x, (mx, 0, mz), zs.at[z, :, edge_tile(x)], xzh.at[n])
+            add(out, OUT, (mx, 0, mz), dxzs.at[n], dxzr.at[n])
             moves.append((mx, 0, mz))
+        moves.append((mx, 0, 0))
     for my, y in STEPS:
-        add(y_in, (0, my, 0), ys.at[y], yh.at[y])
-        add(y_out, (0, my, 0), dys.at[y, :, 0:ci], dyr.at[y])
+        add(y_in, Y_IN, (0, my, 0), ys.at[y], yh.at[y], NUM_FIELDS)
+        add(out, OUT, (0, my, 0), dys.at[y, :, 0:ci], dyr.at[y], NUM_TERMS)
+        for mz, z in STEPS:
+            add(z_in, Z_IN, (0, my, mz), ez.at[z], yzh.at[2 * y + z])
+            add(out, OUT, (0, my, mz), dyzs.at[z], dyzr.at[2 * y + z])
+            moves.append((0, my, mz))
         moves.append((0, my, 0))
-        for mz, z in STEPS:
-            add(z_in, (0, my, mz), ez.at[z], yzh.at[2 * y + z])
-            add(z_out, (0, my, mz), dyzs.at[z], dyzr.at[2 * y + z])
-            moves.append((0, my, mz))
     for mz, z in STEPS:
-        add(z_in, (0, 0, mz), zs.at[z], zh.at[z])
-        add(z_out, (0, 0, mz), dzs.at[z, :, 0:ci], dzr.at[z])
+        add(z_in, Z_IN, (0, 0, mz), zs.at[z], zh.at[z], inner // 128)
+        add(out, OUT, (0, 0, mz), dzs.at[z, :, 0:ci], dzr.at[z], NUM_TERMS)
         moves.append((0, 0, mz))
+    moves.sort(key=lambda move: -sum(abs(step) for step in move))
 
     barrier = pltpu.get_barrier_semaphore()
     for move in moves:
@@ -224,6 +261,10 @@
         def _():
             pl.semaphore_signal(barrier, inc=1, device_id=peer(move), device_id_type=MESH)
 
+    loads = [
+        pltpu.make_async_copy(vel, fields.at[0:3], load_sem.at[0]),
+        pltpu.make_async_copy(sca, fields.at[3:6], load_sem.at[1]),
+    ]
     small = [
         pltpu.make_async_copy(src, dst, load_sem.at[2 + n])
         for n, (src, dst) in enumerate(
@@ -238,66 +279,9 @@
             ]
         )
     ]
-    loads = [
-        pltpu.make_async_copy(vel, fields.at[0:3], load_sem.at[0]),
-        pltpu.make_async_copy(sca, fields.at[3:6], load_sem.at[1]),
-    ]
-    for load in small + loads:
+    for load in loads + small:
         load.start()
-    for message in y_in + z_in + y_out + z_out:
-        message.blank()
-    zs[...] = jnp.zeros_like(zs)
     xys[...] = jnp.zeros_like(xys)
-    dxys[...] = jnp.zeros_like(dxys)
-    dxzs[...] = jnp.zeros_like(dxzs)
-
-    for load in small:
-        load.wait()
-    xa, xb, lx = pair_weights(pos[0:1])
-    ya, yb, ly = pair_weights(pos[1:2])
-    za, zb, lz = pair_weights(pos[2:3])
-    i0 = li[...].astype(F32) + lx
-    j0 = lj[...].astype(F32) + ly
-    k0 = lk[...].astype(F32) + lz
-
-    def at(index, base, wa, wb):
-        return jnp.where(base == index, wa, jnp.where(base + 1.0 == index, wb, 0.0))
-
-    x_low, x_high = at(-1.0, i0, xa, xb), at(float(ci), i0, xa, xb)
-    y_low, y_high = at(-1.0, j0, ya, yb), at(float(cj), j0, ya, yb)
-    z_low, z_high = at(-1.0, k0, za, zb), at(float(ck), k0, za, zb)
-    for n, row in enumerate((x_high, x_low, j0, k0, ya, yb, za, zb)):
-        geo[n : n + 1] = row
-    xt[0:ci] = spots(0, ci, i0, xa, xb)
-    xt[ci : 2 * ci] = jnp.concatenate([x_low, x_high, jnp.zeros((ci - 2, slots), F32)], axis=0)
-    across = spots(0, cj, j0, ya, yb)
-    rims = [
-        jnp.broadcast_to(y_low, (8, slots)),
-        jnp.broadcast_to(y_high, (8, slots)),
-        jnp.zeros((yt_hi.shape[0] - cj - 16, slots), F32),
-    ]
-    yt_hi[...], yt_lo[...] = split(jnp.concatenate([across] + rims, axis=0))
-    for i in range(ci):
-        high, low = split(xt[i : i + 1] * across)
-        w_hi[i * cj : (i + 1) * cj] = high
-        w_lo[i * cj : (i + 1) * cj] = low
-    for n, row in enumerate((x_low, x_high)):
-        high, low = split(row * across)
-        wx[n, 0:cj] = high
-        wx[n, cj : 2 * cj] = high
-        wx[n, 2 * cj : 3 * cj] = low
-    corners = [a * b for a in (x_low, x_high) for b in (y_low, y_high)]
-    sides = [xt[0:ci] * y_low, xt[0:ci] * y_high]
-    group = wy.shape[0] // 4
-    filler = [jnp.zeros((group - 2 * ci - 4, slots), F32)]
-    high, low = split(jnp.concatenate(sides + corners + filler, axis=0))
-    wy[0:group] = high
-    wy[group : 2 * group] = high
-    wy[2 * group : 3 * group] = low
-    wy[3 * group : 4 * group] = jnp.zeros((group, slots), BF16)
-    line[...] = spots(0, ck, k0, za, zb)
-    line_hi[...], line_lo[...] = split(line[...])
-
     for load in loads:
         load.wait()
     for y in range(2):
@@ -306,10 +290,14 @@
         for x in range(2):
             xys[2 * x + y, 0:NUM_FIELDS] = fields[:, face(x, ci), row, :]
     pl.semaphore_wait(barrier, sum(exists(move, 1).astype(jnp.int32) for move in moves))
-
-    for message in x_in + y_in + geo_in:
+    for message in y_in + faces[0] + faces[1]:
         message.start()
 
+    zs[...] = jnp.zeros_like(zs)
+    dxys[...] = jnp.zeros_like(dxys)
+    dxzs[...] = jnp.zeros_like(dxzs)
+    for message in y_in + z_in + rim_in[0] + rim_in[1] + out:
+        message.blank()
     for f in range(NUM_FIELDS):
         turned = fields[f].reshape(inner, ck).T
         high, low = split(turned)
@@ -324,15 +312,71 @@
     chosen = jnp.where(chosen, 1.0, 0.0).astype(BF16)
     high, low = split(zs[...].reshape(16, inner))
     ez[...] = (nn(high, chosen) + nn(low, chosen)).reshape(2, 8, 128)
-    for message in z_in:
+    for message in z_in + rim_in[0] + rim_in[1]:
         message.start()
 
+    for load in small:
+        load.wait()
+    xa, xb, lx = pair_weights(pos[0:1])
+    ya, yb, ly = pair_weights(pos[1:2])
+    za, zb, lz = pair_weights(pos[2:3])
+    i0 = li[...].astype(F32) + lx
+    j0 = lj[...].astype(F32) + ly
+    k0 = lk[...].astype(F32) + lz
+
+    def at(index, base, wa, wb):
+        return jnp.where(base == index, wa, jnp.where(base + 1.0 == index, wb, 0.0))
+
+    x_low, x_high = at(-1.0, i0, xa, xb), at(float(ci), i0, xa, xb)
+    y_low, y_high = at(-1.0, j0, ya, yb), at(float(cj), j0, ya, yb)
+    z_low, z_high = at(-1.0, k0, za, zb), at(float(ck), k0, za, zb)
+    for n, row in enumerate((x_high, x_low, j0, k0, ya, yb, za, zb)):
+        geo[n : n + 1] = row
+    xt[0:ci] = spots(0, ci, i0, xa, xb)
+    xt[ci : 2 * ci] = jnp.concatenate([x_low, x_high, jnp.zeros((ci - 2, slots), F32)], axis=0)
+    across = spots(0, cj, j0, ya, yb)
+    rims = [
+        jnp.broadcast_to(y_low, (8, slots)),
+        jnp.broadcast_to(y_high, (8, slots)),
+        jnp.zeros((128 - cj - 16, slots), F32),
+    ]
+    high, low = split(jnp.concatenate([across] + rims, axis=0))
+    yt[0:128] = high
+    yt[128:256] = low
+    for i in range(ci):
+        high, low = split(xt[i : i + 1] * across)
+        w_hi[i * cj : (i + 1) * cj] = high
+        w_lo[i * cj : (i + 1) * cj] = low
+    for n, row in enumerate((x_low, x_high)):
+        high, low = split(row * across)
+        wx[n, 0:cj] = high
+        wx[n, cj : 2 * cj] = high
+        wx[n, 2 * cj : 3 * cj] = low
+    corners = [a * b for a in (x_low, x_high) for b in (y_low, y_high)]
+    for n, row in enumerate(corners):
+        cw[n : n + 1] = row
+    sides = [xt[0:ci] * y_low, xt[0:ci] * y_high]
+    group = wy.shape[0] // 4
+    filler = [jnp.zeros((group - 2 * ci - 4, slots), F32)]
+    high, low = split(jnp.concatenate(sides + corners + filler, axis=0))
+    wy[0:group] = high
+    wy[group : 2 * group] = high
+    wy[2 * group : 3 * group] = low
+    wy[3 * group : 4 * group] = jnp.zeros((group, slots), BF16)
+    line[...] = spots(0, ck, k0, za, zb)
+    high, low = split(line[...])
+    lines[0:ck] = high
+    lines[ck : 2 * ck] = low
+
+    for message in geo_in:
+        message.start()
+
     width = 256
 
-    def collect(got, here):
+    def collect(got, here, number):
         return [
-            jnp.sum(got[f * ck : (f + 1) * ck] * line[:, here], axis=0, keepdims=True)
-            for f in range(NUM_FIELDS)
+            jnp.sum(got[n * ck : (n + 1) * ck] * line[:, here], axis=0, keepdims=True)
+            for n in range(number)
         ]
 
     for s in range(0, slots, width):
@@ -340,11 +384,10 @@
         got = nn(ft_hi[...], w_hi[:, here])
         got += nn(ft_hi[...], w_lo[:, here])
         got += nn(ft_lo[...], w_hi[:, here])
-        for f, part in enumerate(collect(got, here)):
+        for f, part in enumerate(collect(got, here, NUM_FIELDS)):
             sampled[f : f + 1, here] = part
 
-    for message in y_in:
-        message.arrive()
+    arrive(y_in)
 
     def turn(flats):
         out = []
@@ -353,11 +396,15 @@
             out.append(jnp.concatenate([high, flat - high, high], axis=0).T.astype(BF16))
         return jnp.concatenate(out, axis=0)
 
-    def more(left, right):
+    def more(left, right, span):
+        rest = []
         for s in range(0, slots, width):
             here = slice(s, s + width)
-            for f, part in enumerate(collect(nn(left, right[:, here]), here)):
+            got = nn(left, right[:, here])
+            for f, part in zip(span, collect(got, here, len(span))):
                 sampled[f : f + 1, here] += part
+            rest.append(got[len(span) * ck :])
+        return jnp.concatenate(rest, axis=1) if left.shape[0] > len(span) * ck else None
 
     empty = jnp.zeros((group - 2 * ci - 4, ck), F32)
     left = turn(
@@ -368,10 +415,9 @@
             for f in range(NUM_FIELDS)
         ]
     )
-    more(left, wy[0 : 3 * group])
-
-    for message in z_in:
-        message.arrive()
+    more(left, wy[0 : 3 * group], range(NUM_FIELDS))
+
+    arrive(z_in)
     lanes = lanes_of((8, 128))
     body = lanes < cj
 
@@ -387,28 +433,45 @@
             block = half(zh[z, :, first : first + 128], i * cj % 128 != 0)
             block += pick(yzh[z], cj + i) + pick(yzh[2 + z], cj + 8 + i)
             ztable[z, i] = block
-        for x in range(2):
-            i = face(x, ci)
-            block = half(xzh[2 * x + z], i * cj % 128 != 0)
-            block += pick(xyzh[4 * x + z], cj + i) + pick(xyzh[4 * x + 2 + z], cj + 8 + i)
-            ztable[z, ci + x] = block
-    blocks = ci + 2
-    high, low = split(ztable[...].reshape(2 * blocks * 8, 128))
-    got = nn(high, yt_hi[...]) + nn(high, yt_lo[...]) + nn(low, yt_hi[...])
+    high, low = split(ztable[...].reshape(2 * ci * 8, 128))
+    got = nn(jnp.concatenate([high, low], axis=0), yt[0:128])
+    got = got[0 : 2 * ci * 8] + got[2 * ci * 8 :] + nn(high, yt[128:256])
     for z, rim in enumerate((z_low, z_high)):
         total = None
-        for b in range(blocks):
-            first = (z * blocks + b) * 8
-            part = got[first : first + 8] * xt[b : b + 1]
+        for i in range(ci):
+            first = (z * ci + i) * 8
+            part = got[first : first + 8] * xt[i : i + 1]
             total = part if total is None else total + part
         sampled[...] += total * rim
 
-    for x, message in enumerate(x_in):
-
-        @pl.when(exists(message.move, -1))
+    for x in range(2):
+
+        @pl.when(exists(faces[x][0].move, -1))
         def _():
-            message.copy.wait_recv()
-            more(turn([xh[x, f] for f in range(NUM_FIELDS)]), wx[x])
+            i = face(x, ci)
+            for part in range(PARTS):
+                span = range(part * CHUNK, (part + 1) * CHUNK)
+                faces[x][part].copy.wait_recv()
+                if part < PARTS - 1:
+                    more(turn([xh[x, f] for f in span]), wx[x], span)
+                    continue
+                arrive(rim_in[x])
+                ends = []
+                for z in range(2):
+                    block = half(xzh[2 * x + z], i * cj % 128 != 0)
+                    high = block.astype(BF16).astype(F32)
+                    beside = jnp.where(body, high, pltpu.roll(block - high, cj, 1))
+                    ends.append(jnp.concatenate([beside, high[:, 0:cj]], axis=1))
+                ends = jnp.concatenate(ends, axis=0).astype(BF16)
+                left = jnp.concatenate([turn([xh[x, f] for f in span]), ends], axis=0)
+                rest = more(left, wx[x], span)
+                for z, rim in enumerate((z_low, z_high)):
+                    total = rest[z * 8 : z * 8 + 8]
+                    for y in range(2):
+                        lane = cj + 8 * y + i
+                        tile = xyzh[4 * x + 2 * y + z]
+                        total += tile[:, lane : lane + 1] * cw[2 * x + y : 2 * x + y + 1]
+                    sampled[...] += total * rim
 
     gas = sampled[...]
     live = lanes_of((1, slots)) // TILE < tally[0]
@@ -439,21 +502,23 @@
     def fan(rims):
         return split(jnp.concatenate([piece * rim for rim in rims for piece in pieces], axis=0))
 
-    def both(high, low, right_hi, right_lo):
-        return nt(high, right_hi) + nt(high, right_lo) + nt(low, right_hi)
+    def both(high, low, right):
+        wide = nt(high, right)
+        return wide[:, 0:128] + wide[:, 128:256] + nt(low, right[0:128])
 
     shape = (2, NUM_TERMS, part_rows, 128)
     high, low = fan((y_high, y_low))
-    dys[...] = both(high, low, line_hi[...], line_lo[...]).reshape(shape)
+    dys[...] = both(high, low, lines[...]).reshape(shape)
     for x in range(2):
         row = ci + 1 - x
         for y in range(2):
             for c in range(NUM_TERMS):
                 dxys[2 * x + y, c : c + 1] = dys[y, c, row : row + 1]
-    for message in y_out:
-        message.start()
+    for message in out:
+        if message.move[2] == 0:
+            message.start()
     high, low = fan((z_high, z_low))
-    dzs[...] = both(high, low, yt_hi[...], yt_lo[...]).reshape(shape)
+    dzs[...] = both(high, low, yt[...]).reshape(shape)
     for z in range(2):
         for x in range(2):
             row = ci + 1 - x
@@ -464,19 +529,24 @@
             keep = (lanes == cj + c) | (lanes == cj + 8 + c)
             tile = jnp.where(keep, dzs[z, c, 0:ci], tile)
         dyzs[z] = tile
-    for message in z_out:
-        message.start()
-
-    for c in range(NUM_TERMS):
-        high, low = split(line[...] * terms[c : c + 1])
-        src_hi[c * ck : (c + 1) * ck] = high
-        src_lo[c * ck : (c + 1) * ck] = low
+    for message in out:
+        if message.move[2] != 0:
+            message.start()
+
     for a in range(0, NUM_TERMS, 2):
         b = min(a + 2, NUM_TERMS)
+        for c in range(a, b):
+            high, low = split(line[...] * terms[c : c + 1])
+            src_hi[c * ck : (c + 1) * ck] = high
+            src_lo[c * ck : (c + 1) * ck] = low
         span = slice(a * ck, b * ck)
-        got = nt(w_hi[...], src_hi[span])
-        got += nt(w_hi[...], src_lo[span])
-        got += nt(w_lo[...], src_hi[span])
+        if b - a == 2:
+            got = nt(w_hi[...], src_hi[span])
+            got += nt(w_hi[...], src_lo[span])
+            got += nt(w_lo[...], src_hi[span])
+        else:
+            got = nt(w_hi[...], jnp.concatenate([src_hi[span], src_lo[span]], axis=0))
+            got = got[:, 0:ck] + got[:, ck:] + nt(w_lo[...], src_hi[span])
         for c in range(a, b):
             dep[c] = got[:, (c - a) * ck : (c - a + 1) * ck].reshape(ci, cj, ck)
 
@@ -488,18 +558,18 @@
             places.copy.wait_recv()
             rows = [geor[x, n : n + 1] for n in range(8)]
             there = spots(0, cj, rows[2], rows[4], rows[5]) * rows[x]
-            along_hi, along_lo = split(spots(0, ck, rows[3], rows[6], rows[7]))
+            along = jnp.concatenate(split(spots(0, ck, rows[3], rows[6], rows[7])), axis=0)
             deposits.copy.wait_recv()
             high, low = split(
                 jnp.concatenate([there * termr[x, c : c + 1] for c in range(NUM_TERMS)], axis=0)
             )
-            got = both(high, low, along_hi, along_lo)
+            got = both(high, low, along)
             for c in range(NUM_TERMS):
                 dep[c, plane] += got[c * cj : (c + 1) * cj]
 
-    for message in y_out + z_out:
-        message.arrive()
-    for message in made:
+    arrive(out)
+    drain(send_sem.at[0], made, 1)
+    for message in x_out:
         message.leave()
 
 
@@ -523,20 +593,25 @@
             lane = cj + 8 if y == 0 else cj
             first, second = (dxyzr[4 * x + 2 * y + z, :, lane : lane + 1] for z in range(2))
             corner.append(dxyr[2 * x + y] + at_ends(first, second, lanes))
-    wide = lanes_of((cj, ck))
+    row = lax.broadcasted_iota(jnp.int32, (32, ci * ck), 0)
+    row = jnp.where(row < 16, row, row - 16)
+    lane = jnp.where(row < 8, row * ck, (row - 8) * ck + ck - 1)
+    spot = jnp.where(lanes_of((32, ci * ck)) == lane, 1.0, 0.0).astype(BF16)
     outs = []
     for c in range(terms):
-        turned = []
+        block = []
         for z in range(2):
-            block = dzr[z, c]
+            total = dzr[z, c]
             for x in range(2):
                 plane = 0 if x == 0 else ci - 1
-                block += jnp.where(rows == plane, dxzr[2 * x + z, c : c + 1], 0.0)
-            turned.append(block)
-        turned = jnp.concatenate(turned, axis=0).T
+                total += jnp.where(rows == plane, dxzr[2 * x + z, c : c + 1], 0.0)
+            block.append(total)
+        block = jnp.concatenate(block, axis=0)
+        high = block.astype(BF16).astype(F32)
+        turned = jnp.concatenate([high, block - high], axis=0).T[0:cj].astype(BF16)
+        ends_of = nn(turned, spot)
         for i in range(ci):
-            first, second = turned[0:cj, i : i + 1], turned[0:cj, ci + i : ci + i + 1]
-            dep[c, i] = part[c, i] + at_ends(first, second, wide)
+            dep[c, i] = part[c, i] + ends_of[:, i * ck : (i + 1) * ck]
         for y in range(2):
             row = 0 if y == 0 else cj - 1
             lane = cj + 8 + c if y == 0 else cj + c
@@ -563,7 +638,6 @@
     pin = lambda value: pltpu.with_memory_space_constraint(value, pltpu.HBM)
     tile = (8, 128)
     group = -(-(2 * ci + 4) // 16) * 16
-    messages = 54
     f32 = lambda *shape: pltpu.VMEM(shape, F32)
     i32 = lambda *shape: pltpu.VMEM(shape, jnp.int32)
     b16 = lambda *shape: pltpu.VMEM(shape, BF16)
@@ -584,12 +658,11 @@
         b16(2, 3 * cj, slots),
         b16(4 * group, slots),
         f32(2 * ci, slots),
-        b16(128, slots),
-        b16(128, slots),
+        f32(4, slots),
+        b16(256, slots),
         f32(ck, slots),
-        b16(ck, slots),
-        b16(ck, slots),
-        f32(2, ci + 2, *tile),
+        b16(2 * ck, slots),
+        f32(2, ci, *tile),
         b16(NUM_TERMS * ck, slots),
         b16(NUM_TERMS * ck, slots),
         f32(8, slots),
@@ -613,9 +686,10 @@
         f32(2, NUM_TERMS, 2 * ci, ck),
         f32(4, *tile),
         f32(2, *tile),
+        f32(256, *tile),
         pltpu.SemaphoreType.DMA((9,)),
-        pltpu.SemaphoreType.DMA((messages,)),
-        pltpu.SemaphoreType.DMA((messages,)),
+        pltpu.SemaphoreType.DMA((3,)),
+        pltpu.SemaphoreType.DMA((9 + 2 * PARTS,)),
     ]
     results = (
         struct(NUM_TERMS, ci, cj, ck),

time: 23.6 us -> 19.7 us (0.83)
  Pallas kernels: 21.8 us -> 18.1 us
    pallas_call x1, Pallas kernels: 19.8 us -> 16.7 us  [local(): pl.pallas_call(functools.partial(kernel, counts), out_shape=results, in_s...]
    pallas_call x1, Pallas kernels: 1.99 us -> 1.39 us  [local(): pl.pallas_call(finish, out_shape=results[0:2], in_specs=[vmem] * len(resu...]
where the time goes in v3:
time: 19.7 us; the launch traced here: 19.4 us
  Pallas kernels  18.1 us (92%)
  between operations  1.29 us (7%)
    pallas_call x1, Pallas kernels, local(): pl.pallas_call(functools.partial(kernel, counts), out_shape=results, in_s...  16.7 us
    pallas_call x1, Pallas kernels, local(): pl.pallas_call(finish, out_shape=results[0:2], in_specs=[vmem] * len(resu...  1.39 us

profile of v3, /device:TPU:0, one launch (start us, length us, event | category | flops | bytes accessed | tf_op | source)
XLA Modules:
  0.0 19.4 jit_solution(888963508602790530)
XLA Ops:
  1.3 16.7 %shard_map.113 = (f32[5,8,64,128]{3,2,1,0:T(8,128)S(1)}, f32[5,1024]{1,0:T(8,128)S(1)}, f32[2,5,8,128]{3,2,1,0:T(8,128)S(1)}, f32[4,8,128]{2,1,0:T(8,128)S(1)}, ...) custom-call(f32[3,8,64,128]{3,2,1,0:T(8,128)} %vel.1, ...), custom_call_target="tpu_custom_call" | custom-call | tf_op jit(solution)/shard_map/pallas_call | solution.py:705
  18.0 1.4 %shard_map.114 = (f32[5,8,64,128]{3,2,1,0:T(8,128)}, f32[5,1024]{1,0:T(8,128)}) custom-call(f32[5,8,64,128]{3,2,1,0:T(8,128)S(1)} %get-tuple-element.10.part, f32[5,1024]{1,0:T(8,128)S(1)} %get-tuple-element.11.old, f32[2,5,8,128]{3,2,1,0:T(8,128)S(1)} %get-tuple-element.12.dyr, f32[4,8,128]{2,1,0:T(8,128)S(1)} %get-tuple-element.13.dxyr, ...), custom_call_target="tpu_custom_call" | custom-call | tf_op jit(solution)/shard_map/pallas_call | solution.py:715

commit v4 on v3

--- a/solution.py
+++ b/solution.py
@@ -88,7 +88,6 @@
     w_hi,
     w_lo,
     wx,
-    wy,
     xt,
     cw,
     yt,
@@ -118,14 +117,21 @@
     dzs,
     dxzs,
     dyzs,
+    xs,
+    edges,
+    fan_hi,
+    fan_lo,
     gauge,
     load_sem,
     send_sem,
     recv_sem,
+    near,
+    far,
 ):
     ci, cj, ck = vel.shape[1:]
     slots = heat.shape[1]
     inner = ci * cj
+    y_rows = wx.shape[1] - 3 * cj
     me = [lax.axis_index(axis) for axis in AXES]
 
     def exists(move, sign):
@@ -215,22 +221,19 @@
     Y_IN, Z_IN, OUT, GEO, TERMS, RIM, FACE = 0, 1, 2, 3, 5, 7, 9
     face = lambda n, extent: extent - 1 if n == 0 else 0
     edge_tile = lambda n: pl.ds(face(n, ci) * cj // 128 * 128, 128)
-    moves = []
-    y_in, z_in, geo_in, x_out, out = [], [], [], [], []
+    y_in, xy_in, z_in, yz_in, geo_in, x_out, out = [], [], [], [], [], [], []
     faces, rim_in = [[], []], [[], []]
     for mx, x in STEPS:
         for my, y in STEPS:
-            add(y_in, Y_IN, (mx, my, 0), xys.at[2 * x + y], xyh.at[2 * x + y])
+            add(xy_in, Y_IN, (mx, my, 0), xys.at[2 * x + y], xyh.at[2 * x + y])
             add(out, OUT, (mx, my, 0), dxys.at[2 * x + y], dxyr.at[2 * x + y])
             for mz, z in STEPS:
                 n = 4 * x + 2 * y + z
                 add(rim_in[x], RIM + x, (mx, my, mz), ez.at[z], xyzh.at[n])
                 add(out, OUT, (mx, my, mz), dxzs.at[2 * x + z], dxyzr.at[n])
-                moves.append((mx, my, mz))
-            moves.append((mx, my, 0))
         for part in range(PARTS):
             span = slice(part * CHUNK, (part + 1) * CHUNK)
-            here = fields.at[span, face(x, ci)]
+            here = xs.at[x, span]
             add(faces[x], FACE + PARTS * x + part, (mx, 0, 0), here, xh.at[x, span], CHUNK * cj // 8)
         add(geo_in, GEO + x, (mx, 0, 0), geo, geor.at[x], slots // 128)
         add(x_out, TERMS + x, (mx, 0, 0), terms, termr.at[x], 0, 1 + x)
@@ -238,66 +241,91 @@
             n = 2 * x + z
             add(rim_in[x], RIM + x, (mx, 0, mz), zs.at[z, :, edge_tile(x)], xzh.at[n])
             add(out, OUT, (mx, 0, mz), dxzs.at[n], dxzr.at[n])
-            moves.append((mx, 0, mz))
-        moves.append((mx, 0, 0))
     for my, y in STEPS:
         add(y_in, Y_IN, (0, my, 0), ys.at[y], yh.at[y], NUM_FIELDS)
         add(out, OUT, (0, my, 0), dys.at[y, :, 0:ci], dyr.at[y], NUM_TERMS)
         for mz, z in STEPS:
-            add(z_in, Z_IN, (0, my, mz), ez.at[z], yzh.at[2 * y + z])
+            add(yz_in, Z_IN, (0, my, mz), ez.at[z], yzh.at[2 * y + z])
             add(out, OUT, (0, my, mz), dyzs.at[z], dyzr.at[2 * y + z])
-            moves.append((0, my, mz))
-        moves.append((0, my, 0))
     for mz, z in STEPS:
         add(z_in, Z_IN, (0, 0, mz), zs.at[z], zh.at[z], inner // 128)
         add(out, OUT, (0, 0, mz), dzs.at[z, :, 0:ci], dzr.at[z], NUM_TERMS)
-        moves.append((0, 0, mz))
-    moves.sort(key=lambda move: -sum(abs(step) for step in move))
-
-    barrier = pltpu.get_barrier_semaphore()
-    for move in moves:
-
+
+    def signal(sem, move):
         @pl.when(exists(move, 1))
         def _():
-            pl.semaphore_signal(barrier, inc=1, device_id=peer(move), device_id_type=MESH)
-
-    loads = [
-        pltpu.make_async_copy(vel, fields.at[0:3], load_sem.at[0]),
-        pltpu.make_async_copy(sca, fields.at[3:6], load_sem.at[1]),
-    ]
-    small = [
-        pltpu.make_async_copy(src, dst, load_sem.at[2 + n])
-        for n, (src, dst) in enumerate(
-            [
-                (pos_in, pos),
-                (li_in, li),
-                (lj_in, lj),
-                (lk_in, lk),
-                (mot_in, mot),
-                (heat_in, heat),
-                (size_in, size),
-            ]
-        )
-    ]
-    for load in loads + small:
-        load.start()
+            pl.semaphore_signal(sem, inc=1, device_id=peer(move), device_id_type=MESH)
+
+    def heard(sem, moves):
+        pl.semaphore_wait(sem, sum(exists(move, -1).astype(jnp.int32) for move in moves))
+
+
+    x_moves = [(step, 0, 0) for step, _ in STEPS]
+    y_moves = [(0, step, 0) for step, _ in STEPS]
+    z_moves = [(0, 0, step) for step, _ in STEPS]
+    barrier = pltpu.get_barrier_semaphore()
+    for move in z_moves + x_moves + y_moves:
+        signal(barrier, move)
+
+    def load(src, dst, number):
+        copy = pltpu.make_async_copy(src, dst, load_sem.at[number])
+        copy.start()
+        return copy
+
+    def loaded(whole, number):
+        pltpu.make_async_copy(whole, whole, load_sem.at[number]).wait()
+
+    for x, move in enumerate(x_moves):
+
+        @pl.when(exists(move, 1))
+        def _():
+            load(vel.at[:, face(x, ci)], xs.at[x, 0:3], x)
+            load(sca.at[:, face(x, ci)], xs.at[x, 3:6], x)
+
+    load(vel, fields.at[0:3], 2)
+    load(sca, fields.at[3:6], 2)
+    pairs = [(pos_in, pos), (mot_in, mot), (li_in, li), (lj_in, lj), (lk_in, lk)]
+    pairs += [(heat_in, heat), (size_in, size)]
+    small = [load(src, dst, 3 + n) for n, (src, dst) in enumerate(pairs)]
+
     xys[...] = jnp.zeros_like(xys)
-    for load in loads:
-        load.wait()
+    zs[...] = jnp.zeros_like(zs)
+    dxys[...] = jnp.zeros_like(dxys)
+    dxzs[...] = jnp.zeros_like(dxzs)
+    for message in y_in + xy_in + z_in + yz_in + rim_in[0] + rim_in[1] + out:
+        message.blank()
+    rows = lax.broadcasted_iota(jnp.int32, (inner, 128), 0)
+    cols = lanes_of((inner, 128))
+    target = jnp.where(cols < cj + 8, (cols - cj) * cj + cj - 1, (cols - cj - 8) * cj)
+    chosen = (rows == target) & (cols >= cj) & (cols < cj + 16)
+    edges[...] = jnp.where(chosen, 1.0, 0.0).astype(BF16)
+
+    for x, move in enumerate(x_moves):
+
+        @pl.when(exists(move, 1))
+        def _():
+            loaded(xs.at[x], x)
+
+    heard(barrier, x_moves + y_moves + z_moves)
+    for move in y_moves:
+        signal(near, move)
+    for part in range(PARTS - 1):
+        for x in range(2):
+            faces[x][part].start()
+    loaded(fields, 2)
     for y in range(2):
         row = face(y, cj)
         ys[y] = fields[:, :, row, :]
         for x in range(2):
             xys[2 * x + y, 0:NUM_FIELDS] = fields[:, face(x, ci), row, :]
-    pl.semaphore_wait(barrier, sum(exists(move, 1).astype(jnp.int32) for move in moves))
-    for message in y_in + faces[0] + faces[1]:
+    for message in y_in:
         message.start()
-
-    zs[...] = jnp.zeros_like(zs)
-    dxys[...] = jnp.zeros_like(dxys)
-    dxzs[...] = jnp.zeros_like(dxzs)
-    for message in y_in + z_in + rim_in[0] + rim_in[1] + out:
-        message.blank()
+    heard(near, y_moves)
+    for move in z_moves:
+        signal(far, move)
+    for message in xy_in + [faces[0][PARTS - 1], faces[1][PARTS - 1]]:
+        message.start()
+
     for f in range(NUM_FIELDS):
         turned = fields[f].reshape(inner, ck).T
         high, low = split(turned)
@@ -305,18 +333,16 @@
         ft_lo[f * ck : (f + 1) * ck] = low
         zs[0, f : f + 1] = turned[ck - 1 : ck]
         zs[1, f : f + 1] = turned[0:1]
-    rows = lax.broadcasted_iota(jnp.int32, (inner, 128), 0)
-    cols = lanes_of((inner, 128))
-    target = jnp.where(cols < cj + 8, (cols - cj) * cj + cj - 1, (cols - cj - 8) * cj)
-    chosen = (rows == target) & (cols >= cj) & (cols < cj + 16)
-    chosen = jnp.where(chosen, 1.0, 0.0).astype(BF16)
+    for message in z_in:
+        message.start()
     high, low = split(zs[...].reshape(16, inner))
-    ez[...] = (nn(high, chosen) + nn(low, chosen)).reshape(2, 8, 128)
-    for message in z_in + rim_in[0] + rim_in[1]:
+    ez[...] = (nn(high, edges[...]) + nn(low, edges[...])).reshape(2, 8, 128)
+    heard(far, z_moves)
+    for message in yz_in + rim_in[0] + rim_in[1]:
         message.start()
 
-    for load in small:
-        load.wait()
+    for copy in small:
+        copy.wait()
     xa, xb, lx = pair_weights(pos[0:1])
     ya, yb, ly = pair_weights(pos[1:2])
     za, zb, lz = pair_weights(pos[2:3])
@@ -347,22 +373,21 @@
         high, low = split(xt[i : i + 1] * across)
         w_hi[i * cj : (i + 1) * cj] = high
         w_lo[i * cj : (i + 1) * cj] = low
+    corners = [a * b for a in (x_low, x_high) for b in (y_low, y_high)]
+    for n, row in enumerate(corners):
+        cw[n : n + 1] = row
+    ends = jnp.concatenate([xt[0:ci] * y_low, xt[0:ci] * y_high] + corners, axis=0)
+    high = ends.astype(BF16).astype(F32)
+    filler = jnp.zeros((y_rows - 3 * ends.shape[0], slots), F32)
+    ends = jnp.concatenate([high, high, ends - high, filler], axis=0)
+    first = exists(x_moves[0], -1)
     for n, row in enumerate((x_low, x_high)):
         high, low = split(row * across)
         wx[n, 0:cj] = high
         wx[n, cj : 2 * cj] = high
         wx[n, 2 * cj : 3 * cj] = low
-    corners = [a * b for a in (x_low, x_high) for b in (y_low, y_high)]
-    for n, row in enumerate(corners):
-        cw[n : n + 1] = row
-    sides = [xt[0:ci] * y_low, xt[0:ci] * y_high]
-    group = wy.shape[0] // 4
-    filler = [jnp.zeros((group - 2 * ci - 4, slots), F32)]
-    high, low = split(jnp.concatenate(sides + corners + filler, axis=0))
-    wy[0:group] = high
-    wy[group : 2 * group] = high
-    wy[2 * group : 3 * group] = low
-    wy[3 * group : 4 * group] = jnp.zeros((group, slots), BF16)
+        share = jnp.where(first, 1.0 - n, float(n))
+        wx[n, 3 * cj :] = (ends * share).astype(BF16)
     line[...] = spots(0, ck, k0, za, zb)
     high, low = split(line[...])
     lines[0:ck] = high
@@ -387,14 +412,18 @@
         for f, part in enumerate(collect(got, here, NUM_FIELDS)):
             sampled[f : f + 1, here] = part
 
-    arrive(y_in)
-
-    def turn(flats):
-        out = []
-        for flat in flats:
+
+    def turn(x, f):
+        beyond = xh[x, f]
+        ends = jnp.concatenate(
+            [yh[0, f], yh[1, f]] + [xyh[q, f : f + 1] for q in range(4)], axis=0
+        )
+        parts = []
+        for flat in (beyond, ends):
             high = flat.astype(BF16).astype(F32)
-            out.append(jnp.concatenate([high, flat - high, high], axis=0).T.astype(BF16))
-        return jnp.concatenate(out, axis=0)
+            parts += [high, flat - high, high]
+        parts.append(jnp.zeros((y_rows - 3 * ends.shape[0], ck), F32))
+        return jnp.concatenate(parts, axis=0).T.astype(BF16)
 
     def more(left, right, span):
         rest = []
@@ -406,18 +435,7 @@
             rest.append(got[len(span) * ck :])
         return jnp.concatenate(rest, axis=1) if left.shape[0] > len(span) * ck else None
 
-    empty = jnp.zeros((group - 2 * ci - 4, ck), F32)
-    left = turn(
-        [
-            jnp.concatenate(
-                [yh[0, f], yh[1, f]] + [xyh[q, f : f + 1] for q in range(4)] + [empty], axis=0
-            )
-            for f in range(NUM_FIELDS)
-        ]
-    )
-    more(left, wy[0 : 3 * group], range(NUM_FIELDS))
-
-    arrive(z_in)
+    arrive(z_in + yz_in)
     lanes = lanes_of((8, 128))
     body = lanes < cj
 
@@ -444,6 +462,7 @@
             total = part if total is None else total + part
         sampled[...] += total * rim
 
+    arrive(y_in + xy_in)
     for x in range(2):
 
         @pl.when(exists(faces[x][0].move, -1))
@@ -453,7 +472,7 @@
                 span = range(part * CHUNK, (part + 1) * CHUNK)
                 faces[x][part].copy.wait_recv()
                 if part < PARTS - 1:
-                    more(turn([xh[x, f] for f in span]), wx[x], span)
+                    more(jnp.concatenate([turn(x, f) for f in span], axis=0), wx[x], span)
                     continue
                 arrive(rim_in[x])
                 ends = []
@@ -461,9 +480,10 @@
                     block = half(xzh[2 * x + z], i * cj % 128 != 0)
                     high = block.astype(BF16).astype(F32)
                     beside = jnp.where(body, high, pltpu.roll(block - high, cj, 1))
-                    ends.append(jnp.concatenate([beside, high[:, 0:cj]], axis=1))
+                    beyond = jnp.where(body, high, 0.0)
+                    ends.append(jnp.concatenate([beside, beyond], axis=1))
                 ends = jnp.concatenate(ends, axis=0).astype(BF16)
-                left = jnp.concatenate([turn([xh[x, f] for f in span]), ends], axis=0)
+                left = jnp.concatenate([turn(x, f) for f in span] + [ends], axis=0)
                 rest = more(left, wx[x], span)
                 for z, rim in enumerate((z_low, z_high)):
                     total = rest[z * 8 : z * 8 + 8]
@@ -507,18 +527,9 @@
         return wide[:, 0:128] + wide[:, 128:256] + nt(low, right[0:128])
 
     shape = (2, NUM_TERMS, part_rows, 128)
-    high, low = fan((y_high, y_low))
-    dys[...] = both(high, low, lines[...]).reshape(shape)
-    for x in range(2):
-        row = ci + 1 - x
-        for y in range(2):
-            for c in range(NUM_TERMS):
-                dxys[2 * x + y, c : c + 1] = dys[y, c, row : row + 1]
-    for message in out:
-        if message.move[2] == 0:
-            message.start()
-    high, low = fan((z_high, z_low))
-    dzs[...] = both(high, low, yt[...]).reshape(shape)
+    fan_hi[0], fan_lo[0] = fan((z_high, z_low))
+    fan_hi[1], fan_lo[1] = fan((y_high, y_low))
+    dzs[...] = both(fan_hi[0], fan_lo[0], yt[...]).reshape(shape)
     for z in range(2):
         for x in range(2):
             row = ci + 1 - x
@@ -531,6 +542,15 @@
         dyzs[z] = tile
     for message in out:
         if message.move[2] != 0:
+            message.start()
+    dys[...] = both(fan_hi[1], fan_lo[1], lines[...]).reshape(shape)
+    for x in range(2):
+        row = ci + 1 - x
+        for y in range(2):
+            for c in range(NUM_TERMS):
+                dxys[2 * x + y, c : c + 1] = dys[y, c, row : row + 1]
+    for message in out:
+        if message.move[2] == 0:
             message.start()
 
     for a in range(0, NUM_TERMS, 2):
@@ -637,7 +657,7 @@
     row = lambda value: value.reshape(1, slots)
     pin = lambda value: pltpu.with_memory_space_constraint(value, pltpu.HBM)
     tile = (8, 128)
-    group = -(-(2 * ci + 4) // 16) * 16
+    y_rows = -(-3 * (2 * ci + 4) // 64) * 64
     f32 = lambda *shape: pltpu.VMEM(shape, F32)
     i32 = lambda *shape: pltpu.VMEM(shape, jnp.int32)
     b16 = lambda *shape: pltpu.VMEM(shape, BF16)
@@ -655,8 +675,7 @@
         b16(NUM_FIELDS * ck, inner),
         b16(inner, slots),
         b16(inner, slots),
-        b16(2, 3 * cj, slots),
-        b16(4 * group, slots),
+        b16(2, 3 * cj + y_rows, slots),
         f32(2 * ci, slots),
         f32(4, slots),
         b16(256, slots),
@@ -686,10 +705,16 @@
         f32(2, NUM_TERMS, 2 * ci, ck),
         f32(4, *tile),
         f32(2, *tile),
+        f32(2, NUM_FIELDS, cj, ck),
+        b16(inner, 128),
+        b16(2, 4 * NUM_TERMS * ci, slots),
+        b16(2, 4 * NUM_TERMS * ci, slots),
         f32(256, *tile),
-        pltpu.SemaphoreType.DMA((9,)),
+        pltpu.SemaphoreType.DMA((10,)),
         pltpu.SemaphoreType.DMA((3,)),
         pltpu.SemaphoreType.DMA((9 + 2 * PARTS,)),
+        pltpu.SemaphoreType.REGULAR,
+        pltpu.SemaphoreType.REGULAR,
     ]
     results = (
         struct(NUM_TERMS, ci, cj, ck),

time: 19.7 us -> 18.4 us (0.934)
  Pallas kernels: 18.1 us -> 16.9 us
    pallas_call x1, Pallas kernels: 16.7 us -> 15.6 us  [local(): pl.pallas_call(functools.partial(kernel, counts), out_shape=results, in_s...]
where the time goes in v4:
time: 18.4 us; the launch traced here: 18.2 us
  Pallas kernels  16.9 us (92%)
  between operations  1.29 us (7%)
    pallas_call x1, Pallas kernels, local(): pl.pallas_call(functools.partial(kernel, counts), out_shape=results, in_s...  15.6 us
    pallas_call x1, Pallas kernels, local(): pl.pallas_call(finish, out_shape=results[0:2], in_specs=[vmem] * len(resu...  1.39 us

profile of v4, /device:TPU:0, one launch (start us, length us, event | category | flops | bytes accessed | tf_op | source)
XLA Modules:
  0.0 18.2 jit_solution(2543579861299939338)
XLA Ops:
  1.3 15.6 %shard_map.113 = (f32[5,8,64,128]{3,2,1,0:T(8,128)S(1)}, f32[5,1024]{1,0:T(8,128)S(1)}, f32[2,5,8,128]{3,2,1,0:T(8,128)S(1)}, f32[4,8,128]{2,1,0:T(8,128)S(1)}, ...) custom-call(f32[3,8,64,128]{3,2,1,0:T(8,128)} %vel.1, ...), custom_call_target="tpu_custom_call" | custom-call | tf_op jit(solution)/shard_map/pallas_call | solution.py:730
  16.8 1.4 %shard_map.114 = (f32[5,8,64,128]{3,2,1,0:T(8,128)}, f32[5,1024]{1,0:T(8,128)}) custom-call(f32[5,8,64,128]{3,2,1,0:T(8,128)S(1)} %get-tuple-element.10.part, f32[5,1024]{1,0:T(8,128)S(1)} %get-tuple-element.11.old, f32[2,5,8,128]{3,2,1,0:T(8,128)S(1)} %get-tuple-element.12.dyr, f32[4,8,128]{2,1,0:T(8,128)S(1)} %get-tuple-element.13.dxyr, ...), custom_call_target="tpu_custom_call" | custom-call | tf_op jit(solution)/shard_map/pallas_call | solution.py:740

commit v5 on v4

--- a/solution.py
+++ b/solution.py
@@ -22,8 +22,6 @@
 STEPS = ((1, 0), (-1, 1))
 NUM_TERMS = 5
 NUM_FIELDS = 6
-PARTS = 3
-CHUNK = NUM_FIELDS // PARTS
 
 
 def split(value):
@@ -48,6 +46,11 @@
 
 def lanes_of(shape):
     return lax.broadcasted_iota(jnp.int32, shape, len(shape) - 1)
+
+
+def tent(count, place):
+    rows = lax.broadcasted_iota(jnp.int32, (count, place.shape[1]), 0).astype(F32)
+    return jnp.maximum(0.0, 1.0 - jnp.abs(rows - place))
 
 
 def spots(first, count, base, wa, wb):
@@ -87,19 +90,22 @@
     ft_lo,
     w_hi,
     w_lo,
-    wx,
+    corner,
     xt,
-    cw,
     yt,
     line,
     lines,
-    ztable,
     src_hi,
     src_lo,
     sampled,
     geo,
+    back,
     terms,
-    xh,
+    there,
+    along,
+    alongs,
+    w_there,
+    face_f,
     yh,
     xyh,
     zh,
@@ -107,17 +113,16 @@
     yzh,
     xyzh,
     geor,
+    backr,
     termr,
     ys,
     xys,
     zs,
     ez,
     dys,
-    dxys,
     dzs,
-    dxzs,
     dyzs,
-    xs,
+    dxyzs,
     edges,
     fan_hi,
     fan_lo,
@@ -125,13 +130,11 @@
     load_sem,
     send_sem,
     recv_sem,
-    near,
     far,
 ):
     ci, cj, ck = vel.shape[1:]
     slots = heat.shape[1]
     inner = ci * cj
-    y_rows = wx.shape[1] - 3 * cj
     me = [lax.axis_index(axis) for axis in AXES]
 
     def exists(move, sign):
@@ -218,38 +221,35 @@
         made.append(message)
         group.append(message)
 
-    Y_IN, Z_IN, OUT, GEO, TERMS, RIM, FACE = 0, 1, 2, 3, 5, 7, 9
+    Y_IN, Z_IN, RIM, OUT, GEO, TERMS, BACK = 0, 1, 2, 3, 4, 6, 8
     face = lambda n, extent: extent - 1 if n == 0 else 0
     edge_tile = lambda n: pl.ds(face(n, ci) * cj // 128 * 128, 128)
     y_in, xy_in, z_in, yz_in, geo_in, x_out, out = [], [], [], [], [], [], []
-    faces, rim_in = [[], []], [[], []]
+    rim_in, corner_in, back_in = [], [], []
     for mx, x in STEPS:
         for my, y in STEPS:
             add(xy_in, Y_IN, (mx, my, 0), xys.at[2 * x + y], xyh.at[2 * x + y])
-            add(out, OUT, (mx, my, 0), dxys.at[2 * x + y], dxyr.at[2 * x + y])
+            add(out, OUT, (mx, my, 0), dys.at[y, NUM_TERMS + x], dxyr.at[2 * x + y])
             for mz, z in STEPS:
                 n = 4 * x + 2 * y + z
-                add(rim_in[x], RIM + x, (mx, my, mz), ez.at[z], xyzh.at[n])
-                add(out, OUT, (mx, my, mz), dxzs.at[2 * x + z], dxyzr.at[n])
-        for part in range(PARTS):
-            span = slice(part * CHUNK, (part + 1) * CHUNK)
-            here = xs.at[x, span]
-            add(faces[x], FACE + PARTS * x + part, (mx, 0, 0), here, xh.at[x, span], CHUNK * cj // 8)
-        add(geo_in, GEO + x, (mx, 0, 0), geo, geor.at[x], slots // 128)
-        add(x_out, TERMS + x, (mx, 0, 0), terms, termr.at[x], 0, 1 + x)
+                add(corner_in, RIM, (mx, my, mz), ez.at[z], xyzh.at[n])
+                add(out, OUT, (mx, my, mz), dxyzs.at[n], dxyzr.at[n])
+        add(geo_in, GEO + x, (mx, 0, 0), geo, geor.at[x], 0, 1 + x)
+        add(back_in, BACK + x, (mx, 0, 0), back.at[1 - x], backr.at[x], 0, 3 + x)
+        add(x_out, TERMS + x, (mx, 0, 0), terms, termr.at[x], 0, 5 + x)
         for mz, z in STEPS:
             n = 2 * x + z
-            add(rim_in[x], RIM + x, (mx, 0, mz), zs.at[z, :, edge_tile(x)], xzh.at[n])
-            add(out, OUT, (mx, 0, mz), dxzs.at[n], dxzr.at[n])
+            add(rim_in, RIM, (mx, 0, mz), zs.at[z, :, edge_tile(x)], xzh.at[n])
+            add(out, OUT, (mx, 0, mz), dzs.at[z, NUM_TERMS + x], dxzr.at[n])
     for my, y in STEPS:
         add(y_in, Y_IN, (0, my, 0), ys.at[y], yh.at[y], NUM_FIELDS)
-        add(out, OUT, (0, my, 0), dys.at[y, :, 0:ci], dyr.at[y], NUM_TERMS)
+        add(out, OUT, (0, my, 0), dys.at[y, 0:NUM_TERMS], dyr.at[y], NUM_TERMS)
         for mz, z in STEPS:
             add(yz_in, Z_IN, (0, my, mz), ez.at[z], yzh.at[2 * y + z])
             add(out, OUT, (0, my, mz), dyzs.at[z], dyzr.at[2 * y + z])
     for mz, z in STEPS:
         add(z_in, Z_IN, (0, 0, mz), zs.at[z], zh.at[z], inner // 128)
-        add(out, OUT, (0, 0, mz), dzs.at[z, :, 0:ci], dzr.at[z], NUM_TERMS)
+        add(out, OUT, (0, 0, mz), dzs.at[z, 0:NUM_TERMS], dzr.at[z], NUM_TERMS)
 
     def signal(sem, move):
         @pl.when(exists(move, 1))
@@ -260,39 +260,41 @@
         pl.semaphore_wait(sem, sum(exists(move, -1).astype(jnp.int32) for move in moves))
 
 
+    def turned_rows(flats, total):
+        parts = []
+        for flat in flats:
+            high = flat.astype(BF16).astype(F32)
+            parts += [high, flat - high, high]
+        spare = total - sum(part.shape[0] for part in parts)
+        if spare > 0:
+            parts.append(jnp.zeros((spare, ck), F32))
+        return jnp.concatenate(parts, axis=0).T.astype(BF16)
+
     x_moves = [(step, 0, 0) for step, _ in STEPS]
     y_moves = [(0, step, 0) for step, _ in STEPS]
     z_moves = [(0, 0, step) for step, _ in STEPS]
+    xy_moves = [(mx, my, 0) for mx, _ in STEPS for my, _ in STEPS]
+    met = xy_moves + z_moves + x_moves + y_moves
     barrier = pltpu.get_barrier_semaphore()
-    for move in z_moves + x_moves + y_moves:
+    for move in met:
         signal(barrier, move)
 
     def load(src, dst, number):
-        copy = pltpu.make_async_copy(src, dst, load_sem.at[number])
-        copy.start()
-        return copy
+        pltpu.make_async_copy(src, dst, load_sem.at[number]).start()
 
     def loaded(whole, number):
         pltpu.make_async_copy(whole, whole, load_sem.at[number]).wait()
 
-    for x, move in enumerate(x_moves):
-
-        @pl.when(exists(move, 1))
-        def _():
-            load(vel.at[:, face(x, ci)], xs.at[x, 0:3], x)
-            load(sca.at[:, face(x, ci)], xs.at[x, 3:6], x)
-
-    load(vel, fields.at[0:3], 2)
-    load(sca, fields.at[3:6], 2)
-    pairs = [(pos_in, pos), (mot_in, mot), (li_in, li), (lj_in, lj), (lk_in, lk)]
-    pairs += [(heat_in, heat), (size_in, size)]
-    small = [load(src, dst, 3 + n) for n, (src, dst) in enumerate(pairs)]
+    pairs = [(pos_in, pos), (li_in, li), (lj_in, lj), (lk_in, lk)]
+    pairs += [(mot_in, mot), (heat_in, heat), (size_in, size)]
+    for (src, dst), number in zip(pairs, (1, 2, 2, 2, 3, 4, 4)):
+        load(src, dst, number)
+    load(vel, fields.at[0:3], 0)
+    load(sca, fields.at[3:6], 0)
 
     xys[...] = jnp.zeros_like(xys)
     zs[...] = jnp.zeros_like(zs)
-    dxys[...] = jnp.zeros_like(dxys)
-    dxzs[...] = jnp.zeros_like(dxzs)
-    for message in y_in + xy_in + z_in + yz_in + rim_in[0] + rim_in[1] + out:
+    for message in y_in + xy_in + z_in + yz_in + rim_in + corner_in + out:
         message.blank()
     rows = lax.broadcasted_iota(jnp.int32, (inner, 128), 0)
     cols = lanes_of((inner, 128))
@@ -300,32 +302,38 @@
     chosen = (rows == target) & (cols >= cj) & (cols < cj + 16)
     edges[...] = jnp.where(chosen, 1.0, 0.0).astype(BF16)
 
-    for x, move in enumerate(x_moves):
-
-        @pl.when(exists(move, 1))
-        def _():
-            loaded(xs.at[x], x)
-
-    heard(barrier, x_moves + y_moves + z_moves)
-    for move in y_moves:
-        signal(near, move)
-    for part in range(PARTS - 1):
-        for x in range(2):
-            faces[x][part].start()
-    loaded(fields, 2)
+    loaded(pos, 1)
+    loaded(gauge.at[0 : 3 * slots // 1024], 2)
+    xa, xb, lx = pair_weights(pos[0:1])
+    ya, yb, ly = pair_weights(pos[1:2])
+    za, zb, lz = pair_weights(pos[2:3])
+    i0 = li[...].astype(F32) + lx
+    j0 = lj[...].astype(F32) + ly
+    k0 = lk[...].astype(F32) + lz
+
+    def at(index, base, wa, wb):
+        return jnp.where(base == index, wa, jnp.where(base + 1.0 == index, wb, 0.0))
+
+    x_low, x_high = at(-1.0, i0, xa, xb), at(float(ci), i0, xa, xb)
+    y_low, y_high = at(-1.0, j0, ya, yb), at(float(cj), j0, ya, yb)
+    z_low, z_high = at(-1.0, k0, za, zb), at(float(ck), k0, za, zb)
+    y_place = lj[...].astype(F32) + pos[1:2]
+    z_place = lk[...].astype(F32) + pos[2:3]
+    for n, row in enumerate((x_high, x_low, y_place, z_place)):
+        geo[n : n + 1] = row
+    heard(barrier, met)
+    for move in z_moves:
+        signal(far, move)
+    for message in geo_in:
+        message.start()
+    loaded(fields, 0)
     for y in range(2):
         row = face(y, cj)
         ys[y] = fields[:, :, row, :]
         for x in range(2):
             xys[2 * x + y, 0:NUM_FIELDS] = fields[:, face(x, ci), row, :]
-    for message in y_in:
+    for message in xy_in + y_in:
         message.start()
-    heard(near, y_moves)
-    for move in z_moves:
-        signal(far, move)
-    for message in xy_in + [faces[0][PARTS - 1], faces[1][PARTS - 1]]:
-        message.start()
-
     for f in range(NUM_FIELDS):
         turned = fields[f].reshape(inner, ck).T
         high, low = split(turned)
@@ -337,27 +345,14 @@
         message.start()
     high, low = split(zs[...].reshape(16, inner))
     ez[...] = (nn(high, edges[...]) + nn(low, edges[...])).reshape(2, 8, 128)
-    heard(far, z_moves)
-    for message in yz_in + rim_in[0] + rim_in[1]:
-        message.start()
-
-    for copy in small:
-        copy.wait()
-    xa, xb, lx = pair_weights(pos[0:1])
-    ya, yb, ly = pair_weights(pos[1:2])
-    za, zb, lz = pair_weights(pos[2:3])
-    i0 = li[...].astype(F32) + lx
-    j0 = lj[...].astype(F32) + ly
-    k0 = lk[...].astype(F32) + lz
-
-    def at(index, base, wa, wb):
-        return jnp.where(base == index, wa, jnp.where(base + 1.0 == index, wb, 0.0))
-
-    x_low, x_high = at(-1.0, i0, xa, xb), at(float(ci), i0, xa, xb)
-    y_low, y_high = at(-1.0, j0, ya, yb), at(float(cj), j0, ya, yb)
-    z_low, z_high = at(-1.0, k0, za, zb), at(float(ck), k0, za, zb)
-    for n, row in enumerate((x_high, x_low, j0, k0, ya, yb, za, zb)):
-        geo[n : n + 1] = row
+    for x in range(2):
+        plane = 0 if x == 0 else ci - 1
+
+        @pl.when(exists(x_moves[x], -1))
+        def _():
+            for f in range(NUM_FIELDS):
+                face_f[x, f * ck : (f + 1) * ck] = turned_rows([fields[f, plane]], 0)
+
     xt[0:ci] = spots(0, ci, i0, xa, xb)
     xt[ci : 2 * ci] = jnp.concatenate([x_low, x_high, jnp.zeros((ci - 2, slots), F32)], axis=0)
     across = spots(0, cj, j0, ya, yb)
@@ -369,71 +364,92 @@
     high, low = split(jnp.concatenate([across] + rims, axis=0))
     yt[0:128] = high
     yt[128:256] = low
+    corners = [a * b for a in (x_low, x_high) for b in (y_low, y_high)]
+    for n, row in enumerate(corners):
+        corner[n : n + 1] = row
+    line[...] = spots(0, ck, k0, za, zb)
+    high, low = split(line[...])
+    lines[0:ck] = high
+    lines[ck : 2 * ck] = low
+
     for i in range(ci):
         high, low = split(xt[i : i + 1] * across)
         w_hi[i * cj : (i + 1) * cj] = high
         w_lo[i * cj : (i + 1) * cj] = low
-    corners = [a * b for a in (x_low, x_high) for b in (y_low, y_high)]
-    for n, row in enumerate(corners):
-        cw[n : n + 1] = row
-    ends = jnp.concatenate([xt[0:ci] * y_low, xt[0:ci] * y_high] + corners, axis=0)
-    high = ends.astype(BF16).astype(F32)
-    filler = jnp.zeros((y_rows - 3 * ends.shape[0], slots), F32)
-    ends = jnp.concatenate([high, high, ends - high, filler], axis=0)
-    first = exists(x_moves[0], -1)
-    for n, row in enumerate((x_low, x_high)):
-        high, low = split(row * across)
-        wx[n, 0:cj] = high
-        wx[n, cj : 2 * cj] = high
-        wx[n, 2 * cj : 3 * cj] = low
-        share = jnp.where(first, 1.0 - n, float(n))
-        wx[n, 3 * cj :] = (ends * share).astype(BF16)
-    line[...] = spots(0, ck, k0, za, zb)
-    high, low = split(line[...])
-    lines[0:ck] = high
-    lines[ck : 2 * ck] = low
-
-    for message in geo_in:
+
+    heard(far, z_moves)
+    for message in corner_in + rim_in + yz_in:
         message.start()
 
     width = 256
 
-    def collect(got, here, number):
-        return [
-            jnp.sum(got[n * ck : (n + 1) * ck] * line[:, here], axis=0, keepdims=True)
-            for n in range(number)
+    def collect(got, table, here, target, start=0):
+        parts = [
+            jnp.sum(got[n * ck : (n + 1) * ck] * table[:, here], axis=0, keepdims=True)
+            for n in range(got.shape[0] // ck)
         ]
-
-    for s in range(0, slots, width):
-        here = slice(s, s + width)
-        got = nn(ft_hi[...], w_hi[:, here])
-        got += nn(ft_hi[...], w_lo[:, here])
-        got += nn(ft_lo[...], w_hi[:, here])
-        for f, part in enumerate(collect(got, here, NUM_FIELDS)):
-            sampled[f : f + 1, here] = part
-
-
-    def turn(x, f):
-        beyond = xh[x, f]
-        ends = jnp.concatenate(
-            [yh[0, f], yh[1, f]] + [xyh[q, f : f + 1] for q in range(4)], axis=0
-        )
-        parts = []
-        for flat in (beyond, ends):
-            high = flat.astype(BF16).astype(F32)
-            parts += [high, flat - high, high]
-        parts.append(jnp.zeros((y_rows - 3 * ends.shape[0], ck), F32))
-        return jnp.concatenate(parts, axis=0).T.astype(BF16)
-
-    def more(left, right, span):
-        rest = []
-        for s in range(0, slots, width):
-            here = slice(s, s + width)
-            got = nn(left, right[:, here])
-            for f, part in zip(span, collect(got, here, len(span))):
-                sampled[f : f + 1, here] += part
-            rest.append(got[len(span) * ck :])
-        return jnp.concatenate(rest, axis=1) if left.shape[0] > len(span) * ck else None
+        for n, part in enumerate(parts):
+            target(start + n, here, part)
+
+    def put(f, here, value):
+        sampled[f : f + 1, here] = value
+
+    def sample(blocks):
+        for s in blocks:
+            here = slice(s * width, (s + 1) * width)
+            for start in range(0, NUM_FIELDS, NUM_FIELDS // 2):
+                part = slice(start * ck, (start + NUM_FIELDS // 2) * ck)
+                got = nn(ft_hi[part], w_hi[:, here])
+                got += nn(ft_hi[part], w_lo[:, here])
+                got += nn(ft_lo[part], w_hi[:, here])
+                collect(got, line, here, put, start)
+
+    sample(range(1))
+    for x, places in enumerate(geo_in):
+
+        @pl.when(exists(places.move, -1))
+        def _():
+            places.copy.wait_recv()
+            there[x] = tent(cj, geor[x, 2:3]) * geor[x, x : x + 1]
+            along[...] = tent(ck, geor[x, 3:4])
+            high, low = split(along[...])
+            alongs[x, 0:ck] = high
+            alongs[x, ck : 2 * ck] = low
+            high, low = split(there[x])
+            w_there[0:cj] = high
+            w_there[cj : 2 * cj] = high
+            w_there[2 * cj : 3 * cj] = low
+
+            def keep(f, here, value):
+                back[x, f : f + 1, here] = value
+
+            for s in range(0, slots, width):
+                here = slice(s, s + width)
+                collect(nn(face_f[x], w_there[:, here]), along, here, keep)
+            back_in[1 - x].copy.start()
+
+    sample(range(1, slots // width))
+    arrive(y_in + xy_in)
+    flat = NUM_FIELDS * ci
+    ends = jnp.concatenate(
+        [yh[y].reshape(flat, ck) for y in range(2)] + [xyh[q] for q in range(4)], axis=0
+    )
+    count = ends.shape[0]
+    high, low = split(ends)
+    got = nn(jnp.concatenate([high, low], axis=0), lines[0:ck])
+    got = got[0:count] + got[count:] + nn(high, lines[ck : 2 * ck])
+    rest = None
+    for q in range(4):
+        first = 2 * flat + q * 8
+        part = got[first : first + 8] * corner[q : q + 1]
+        rest = part if rest is None else rest + part
+    for f in range(NUM_FIELDS):
+        total = sampled[f : f + 1] + rest[f : f + 1]
+        for y, rim in enumerate((y_low, y_high)):
+            first = y * flat + f * ci
+            part = got[first : first + ci] * xt[0:ci]
+            total += jnp.sum(part, axis=0, keepdims=True) * rim
+        sampled[f : f + 1] = total
 
     arrive(z_in + yz_in)
     lanes = lanes_of((8, 128))
@@ -445,53 +461,44 @@
     def pick(tile, lane):
         return jnp.where(lanes == lane, tile, 0.0)
 
+    def beyond(blocks, planes):
+        count = 2 * planes.shape[0] * 8
+        high, low = split(jnp.concatenate(blocks, axis=0))
+        got = nn(jnp.concatenate([high, low], axis=0), yt[0:128])
+        got = got[0:count] + got[count:] + nn(high, yt[128:256])
+        for z, rim in enumerate((z_low, z_high)):
+            total = None
+            for b in range(planes.shape[0]):
+                first = (z * planes.shape[0] + b) * 8
+                part = got[first : first + 8] * planes[b : b + 1]
+                total = part if total is None else total + part
+            sampled[...] += total * rim
+
+    blocks = []
     for z in range(2):
         for i in range(ci):
             first = i * cj // 128 * 128
             block = half(zh[z, :, first : first + 128], i * cj % 128 != 0)
-            block += pick(yzh[z], cj + i) + pick(yzh[2 + z], cj + 8 + i)
-            ztable[z, i] = block
-    high, low = split(ztable[...].reshape(2 * ci * 8, 128))
-    got = nn(jnp.concatenate([high, low], axis=0), yt[0:128])
-    got = got[0 : 2 * ci * 8] + got[2 * ci * 8 :] + nn(high, yt[128:256])
-    for z, rim in enumerate((z_low, z_high)):
-        total = None
-        for i in range(ci):
-            first = (z * ci + i) * 8
-            part = got[first : first + 8] * xt[i : i + 1]
-            total = part if total is None else total + part
-        sampled[...] += total * rim
-
-    arrive(y_in + xy_in)
-    for x in range(2):
-
-        @pl.when(exists(faces[x][0].move, -1))
+            blocks.append(block + pick(yzh[z], cj + i) + pick(yzh[2 + z], cj + 8 + i))
+    beyond(blocks, xt[0:ci])
+    loaded(mot, 3)
+    loaded(gauge.at[0 : 2 * slots // 1024], 4)
+    for x, message in enumerate(back_in):
+
+        @pl.when(exists(message.move, -1))
         def _():
+            message.copy.wait_recv()
+            sampled[0:NUM_FIELDS] += backr[x]
+
+    arrive(rim_in + corner_in)
+    blocks = []
+    for z in range(2):
+        for x in range(2):
             i = face(x, ci)
-            for part in range(PARTS):
-                span = range(part * CHUNK, (part + 1) * CHUNK)
-                faces[x][part].copy.wait_recv()
-                if part < PARTS - 1:
-                    more(jnp.concatenate([turn(x, f) for f in span], axis=0), wx[x], span)
-                    continue
-                arrive(rim_in[x])
-                ends = []
-                for z in range(2):
-                    block = half(xzh[2 * x + z], i * cj % 128 != 0)
-                    high = block.astype(BF16).astype(F32)
-                    beside = jnp.where(body, high, pltpu.roll(block - high, cj, 1))
-                    beyond = jnp.where(body, high, 0.0)
-                    ends.append(jnp.concatenate([beside, beyond], axis=1))
-                ends = jnp.concatenate(ends, axis=0).astype(BF16)
-                left = jnp.concatenate([turn(x, f) for f in span] + [ends], axis=0)
-                rest = more(left, wx[x], span)
-                for z, rim in enumerate((z_low, z_high)):
-                    total = rest[z * 8 : z * 8 + 8]
-                    for y in range(2):
-                        lane = cj + 8 * y + i
-                        tile = xyzh[4 * x + 2 * y + z]
-                        total += tile[:, lane : lane + 1] * cw[2 * x + y : 2 * x + y + 1]
-                    sampled[...] += total * rim
+            block = half(xzh[2 * x + z], i * cj % 128 != 0)
+            block += pick(xyzh[4 * x + z], cj + i) + pick(xyzh[4 * x + 2 + z], cj + 8 + i)
+            blocks.append(block)
+    beyond(blocks, xt[ci : ci + 2])
 
     gas = sampled[...]
     live = lanes_of((1, slots)) // TILE < tally[0]
@@ -516,8 +523,22 @@
     for message in x_out:
         message.start()
 
-    part_rows = 2 * ci
-    pieces = [xt[...] * terms[c : c + 1] for c in range(NUM_TERMS)]
+    stack = jnp.concatenate(
+        [terms[...], jnp.zeros((8 - NUM_TERMS, slots), F32)], axis=0
+    )
+    for x in range(2):
+        for y in range(2):
+            row = 2 * (1 - x) + 1 - y
+            for z, rim in enumerate((z_high, z_low)):
+                part = stack * (corner[row : row + 1] * rim)
+                part = jnp.sum(part, axis=1, keepdims=True)
+                dxyzs[4 * x + 2 * y + z] = jnp.broadcast_to(part, (8, 128))
+    for message in out:
+        if 0 not in message.move:
+            message.start()
+
+    pieces = [xt[0:ci] * terms[c : c + 1] for c in range(NUM_TERMS)]
+    pieces += [stack * xt[ci + 1 - x : ci + 2 - x] for x in range(2)]
 
     def fan(rims):
         return split(jnp.concatenate([piece * rim for rim in rims for piece in pieces], axis=0))
@@ -526,29 +547,20 @@
         wide = nt(high, right)
         return wide[:, 0:128] + wide[:, 128:256] + nt(low, right[0:128])
 
-    shape = (2, NUM_TERMS, part_rows, 128)
+    shape = (2, NUM_TERMS + 2, ci, 128)
     fan_hi[0], fan_lo[0] = fan((z_high, z_low))
-    fan_hi[1], fan_lo[1] = fan((y_high, y_low))
     dzs[...] = both(fan_hi[0], fan_lo[0], yt[...]).reshape(shape)
     for z in range(2):
-        for x in range(2):
-            row = ci + 1 - x
-            for c in range(NUM_TERMS):
-                dxzs[2 * x + z, c : c + 1] = dzs[z, c, row : row + 1]
         tile = jnp.zeros((8, 128), F32)
         for c in range(NUM_TERMS):
             keep = (lanes == cj + c) | (lanes == cj + 8 + c)
-            tile = jnp.where(keep, dzs[z, c, 0:ci], tile)
+            tile = jnp.where(keep, dzs[z, c], tile)
         dyzs[z] = tile
     for message in out:
-        if message.move[2] != 0:
+        if message.move[2] != 0 and 0 in message.move:
             message.start()
+    fan_hi[1], fan_lo[1] = fan((y_high, y_low))
     dys[...] = both(fan_hi[1], fan_lo[1], lines[...]).reshape(shape)
-    for x in range(2):
-        row = ci + 1 - x
-        for y in range(2):
-            for c in range(NUM_TERMS):
-                dxys[2 * x + y, c : c + 1] = dys[y, c, row : row + 1]
     for message in out:
         if message.move[2] == 0:
             message.start()
@@ -570,26 +582,22 @@
         for c in range(a, b):
             dep[c] = got[:, (c - a) * ck : (c - a + 1) * ck].reshape(ci, cj, ck)
 
-    for x, (places, deposits) in enumerate(zip(geo_in, x_out)):
+    for x, deposits in enumerate(x_out):
         plane = 0 if x == 0 else ci - 1
 
-        @pl.when(exists(places.move, -1))
+        @pl.when(exists(deposits.move, -1))
         def _():
-            places.copy.wait_recv()
-            rows = [geor[x, n : n + 1] for n in range(8)]
-            there = spots(0, cj, rows[2], rows[4], rows[5]) * rows[x]
-            along = jnp.concatenate(split(spots(0, ck, rows[3], rows[6], rows[7])), axis=0)
             deposits.copy.wait_recv()
             high, low = split(
-                jnp.concatenate([there * termr[x, c : c + 1] for c in range(NUM_TERMS)], axis=0)
+                jnp.concatenate([there[x] * termr[x, c : c + 1] for c in range(NUM_TERMS)], axis=0)
             )
-            got = both(high, low, along)
+            got = both(high, low, alongs[x])
             for c in range(NUM_TERMS):
                 dep[c, plane] += got[c * cj : (c + 1) * cj]
 
     arrive(out)
     drain(send_sem.at[0], made, 1)
-    for message in x_out:
+    for message in geo_in + back_in + x_out:
         message.leave()
 
 
@@ -657,7 +665,6 @@
     row = lambda value: value.reshape(1, slots)
     pin = lambda value: pltpu.with_memory_space_constraint(value, pltpu.HBM)
     tile = (8, 128)
-    y_rows = -(-3 * (2 * ci + 4) // 64) * 64
     f32 = lambda *shape: pltpu.VMEM(shape, F32)
     i32 = lambda *shape: pltpu.VMEM(shape, jnp.int32)
     b16 = lambda *shape: pltpu.VMEM(shape, BF16)
@@ -675,45 +682,46 @@
         b16(NUM_FIELDS * ck, inner),
         b16(inner, slots),
         b16(inner, slots),
-        b16(2, 3 * cj + y_rows, slots),
+        f32(4, slots),
         f32(2 * ci, slots),
-        f32(4, slots),
         b16(256, slots),
         f32(ck, slots),
         b16(2 * ck, slots),
-        f32(2, ci, *tile),
         b16(NUM_TERMS * ck, slots),
         b16(NUM_TERMS * ck, slots),
         f32(8, slots),
-        f32(8, slots),
+        f32(4, slots),
+        f32(2, NUM_FIELDS, slots),
         f32(NUM_TERMS, slots),
-        f32(2, NUM_FIELDS, cj, ck),
+        f32(2, cj, slots),
+        f32(ck, slots),
+        b16(2, 2 * ck, slots),
+        b16(3 * cj, slots),
+        b16(2, NUM_FIELDS * ck, 3 * cj),
         f32(2, NUM_FIELDS, ci, ck),
         f32(4, *tile),
         f32(2, 8, inner),
         f32(4, *tile),
         f32(4, *tile),
         f32(8, *tile),
-        f32(2, 8, slots),
+        f32(2, 4, slots),
+        f32(2, NUM_FIELDS, slots),
         f32(2, NUM_TERMS, slots),
         f32(2, NUM_FIELDS, ci, ck),
         f32(4, *tile),
         f32(2, 8, inner),
         f32(2, *tile),
-        f32(2, NUM_TERMS, 2 * ci, ck),
-        f32(4, *tile),
-        f32(2, NUM_TERMS, 2 * ci, ck),
-        f32(4, *tile),
+        f32(2, NUM_TERMS + 2, ci, ck),
+        f32(2, NUM_TERMS + 2, ci, ck),
         f32(2, *tile),
-        f32(2, NUM_FIELDS, cj, ck),
+        f32(8, *tile),
         b16(inner, 128),
-        b16(2, 4 * NUM_TERMS * ci, slots),
-        b16(2, 4 * NUM_TERMS * ci, slots),
+        b16(2, 2 * (NUM_TERMS + 2) * ci, slots),
+        b16(2, 2 * (NUM_TERMS + 2) * ci, slots),
         f32(256, *tile),
+        pltpu.SemaphoreType.DMA((5,)),
+        pltpu.SemaphoreType.DMA((7,)),
         pltpu.SemaphoreType.DMA((10,)),
-        pltpu.SemaphoreType.DMA((3,)),
-        pltpu.SemaphoreType.DMA((9 + 2 * PARTS,)),
-        pltpu.SemaphoreType.REGULAR,
         pltpu.SemaphoreType.REGULAR,
     ]
     results = (

time: 18.4 us -> 17.6 us (0.957)
  Pallas kernels: 16.9 us -> 16 us
    pallas_call x1, Pallas kernels: 15.6 us -> 14.6 us  [local(): pl.pallas_call(functools.partial(kernel, counts), out_shape=results, in_s...]
where the time goes in v5:
time: 17.6 us; the launch traced here: 17.3 us
  Pallas kernels  16 us (91%)
  between operations  1.29 us (7%)
    pallas_call x1, Pallas kernels, local(): pl.pallas_call(functools.partial(kernel, counts), out_shape=results, in_s...  14.6 us
    pallas_call x1, Pallas kernels, local(): pl.pallas_call(finish, out_shape=results[0:2], in_specs=[vmem] * len(resu...  1.39 us

profile of v5, /device:TPU:0, one launch (start us, length us, event | category | flops | bytes accessed | tf_op | source)
XLA Modules:
  0.0 17.3 jit_solution(2106213570522355769)
XLA Ops:
  1.3 14.6 %shard_map.113 = (f32[5,8,64,128]{3,2,1,0:T(8,128)S(1)}, f32[5,1024]{1,0:T(8,128)S(1)}, f32[2,5,8,128]{3,2,1,0:T(8,128)S(1)}, f32[4,8,128]{2,1,0:T(8,128)S(1)}, ...) custom-call(f32[3,8,64,128]{3,2,1,0:T(8,128)} %vel.1, ...), custom_call_target="tpu_custom_call" | custom-call | tf_op jit(solution)/shard_map/pallas_call | solution.py:738
  15.9 1.4 %shard_map.114 = (f32[5,8,64,128]{3,2,1,0:T(8,128)}, f32[5,1024]{1,0:T(8,128)}) custom-call(f32[5,8,64,128]{3,2,1,0:T(8,128)S(1)} %get-tuple-element.10.part, f32[5,1024]{1,0:T(8,128)S(1)} %get-tuple-element.11.old, f32[2,5,8,128]{3,2,1,0:T(8,128)S(1)} %get-tuple-element.12.dyr, f32[4,8,128]{2,1,0:T(8,128)S(1)} %get-tuple-element.13.dxyr, ...), custom_call_target="tpu_custom_call" | custom-call | tf_op jit(solution)/shard_map/pallas_call | solution.py:748

commit v6 on v5

--- a/solution.py
+++ b/solution.py
@@ -321,6 +321,29 @@
     z_place = lk[...].astype(F32) + pos[2:3]
     for n, row in enumerate((x_high, x_low, y_place, z_place)):
         geo[n : n + 1] = row
+    xt[0:ci] = spots(0, ci, i0, xa, xb)
+    xt[ci : 2 * ci] = jnp.concatenate([x_low, x_high, jnp.zeros((ci - 2, slots), F32)], axis=0)
+    across = spots(0, cj, j0, ya, yb)
+    rims = [
+        jnp.broadcast_to(y_low, (8, slots)),
+        jnp.broadcast_to(y_high, (8, slots)),
+        jnp.zeros((128 - cj - 16, slots), F32),
+    ]
+    high, low = split(jnp.concatenate([across] + rims, axis=0))
+    yt[0:128] = high
+    yt[128:256] = low
+    corners = [a * b for a in (x_low, x_high) for b in (y_low, y_high)]
+    for n, row in enumerate(corners):
+        corner[n : n + 1] = row
+    line[...] = spots(0, ck, k0, za, zb)
+    high, low = split(line[...])
+    lines[0:ck] = high
+    lines[ck : 2 * ck] = low
+
+    for i in range(ci):
+        high, low = split(xt[i : i + 1] * across)
+        w_hi[i * cj : (i + 1) * cj] = high
+        w_lo[i * cj : (i + 1) * cj] = low
     heard(barrier, met)
     for move in z_moves:
         signal(far, move)
@@ -353,34 +376,6 @@
             for f in range(NUM_FIELDS):
                 face_f[x, f * ck : (f + 1) * ck] = turned_rows([fields[f, plane]], 0)
 
-    xt[0:ci] = spots(0, ci, i0, xa, xb)
-    xt[ci : 2 * ci] = jnp.concatenate([x_low, x_high, jnp.zeros((ci - 2, slots), F32)], axis=0)
-    across = spots(0, cj, j0, ya, yb)
-    rims = [
-        jnp.broadcast_to(y_low, (8, slots)),
-        jnp.broadcast_to(y_high, (8, slots)),
-        jnp.zeros((128 - cj - 16, slots), F32),
-    ]
-    high, low = split(jnp.concatenate([across] + rims, axis=0))
-    yt[0:128] = high
-    yt[128:256] = low
-    corners = [a * b for a in (x_low, x_high) for b in (y_low, y_high)]
-    for n, row in enumerate(corners):
-        corner[n : n + 1] = row
-    line[...] = spots(0, ck, k0, za, zb)
-    high, low = split(line[...])
-    lines[0:ck] = high
-    lines[ck : 2 * ck] = low
-
-    for i in range(ci):
-        high, low = split(xt[i : i + 1] * across)
-        w_hi[i * cj : (i + 1) * cj] = high
-        w_lo[i * cj : (i + 1) * cj] = low
-
-    heard(far, z_moves)
-    for message in corner_in + rim_in + yz_in:
-        message.start()
-
     width = 256
 
     def collect(got, table, here, target, start=0):
@@ -404,31 +399,49 @@
                 got += nn(ft_lo[part], w_hi[:, here])
                 collect(got, line, here, put, start)
 
+    def ghosts():
+        for x, places in enumerate(geo_in):
+
+            @pl.when(exists(places.move, -1))
+            def _():
+                places.copy.wait_recv()
+                there[x] = tent(cj, geor[x, 2:3]) * geor[x, x : x + 1]
+                along[...] = tent(ck, geor[x, 3:4])
+                high, low = split(along[...])
+                alongs[x, 0:ck] = high
+                alongs[x, ck : 2 * ck] = low
+                high, low = split(there[x])
+                w_there[0:cj] = high
+                w_there[cj : 2 * cj] = high
+                w_there[2 * cj : 3 * cj] = low
+
+                def keep(f, here, value):
+                    back[x, f : f + 1, here] = value
+
+                for s in range(0, slots, width):
+                    here = slice(s, s + width)
+                    collect(nn(face_f[x], w_there[:, here]), along, here, keep)
+                back_in[1 - x].copy.start()
+
     sample(range(1))
-    for x, places in enumerate(geo_in):
-
-        @pl.when(exists(places.move, -1))
-        def _():
-            places.copy.wait_recv()
-            there[x] = tent(cj, geor[x, 2:3]) * geor[x, x : x + 1]
-            along[...] = tent(ck, geor[x, 3:4])
-            high, low = split(along[...])
-            alongs[x, 0:ck] = high
-            alongs[x, ck : 2 * ck] = low
-            high, low = split(there[x])
-            w_there[0:cj] = high
-            w_there[cj : 2 * cj] = high
-            w_there[2 * cj : 3 * cj] = low
-
-            def keep(f, here, value):
-                back[x, f : f + 1, here] = value
-
-            for s in range(0, slots, width):
-                here = slice(s, s + width)
-                collect(nn(face_f[x], w_there[:, here]), along, here, keep)
-            back_in[1 - x].copy.start()
-
-    sample(range(1, slots // width))
+    heard(far, z_moves)
+    for message in corner_in + rim_in + yz_in:
+        message.start()
+
+    early = lax.rem(me[0], 2) == 1
+    blocks = slots // width
+
+    @pl.when(early)
+    def _():
+        ghosts()
+        sample(range(1, blocks))
+
+    @pl.when(jnp.logical_not(early))
+    def _():
+        sample(range(1, blocks // 2))
+        ghosts()
+        sample(range(blocks // 2, blocks))
+
     arrive(y_in + xy_in)
     flat = NUM_FIELDS * ci
     ends = jnp.concatenate(

time: 17.6 us -> 17.6 us (level)
  no operation moved by 1% of the time
where the time goes in v6:
time: 17.6 us; the launch traced here: 17.3 us
  Pallas kernels  16 us (91%)
  between operations  1.29 us (7%)
    pallas_call x1, Pallas kernels, local(): pl.pallas_call(functools.partial(kernel, counts), out_shape=results, in_s...  14.6 us
    pallas_call x1, Pallas kernels, local(): pl.pallas_call(finish, out_shape=results[0:2], in_specs=[vmem] * len(resu...  1.39 us

profile of v6, /device:TPU:0, one launch (start us, length us, event | category | flops | bytes accessed | tf_op | source)
XLA Modules:
  0.0 17.3 jit_solution(1494788882197963908)
XLA Ops:
  1.3 14.6 %shard_map.113 = (f32[5,8,64,128]{3,2,1,0:T(8,128)S(1)}, f32[5,1024]{1,0:T(8,128)S(1)}, f32[2,5,8,128]{3,2,1,0:T(8,128)S(1)}, f32[4,8,128]{2,1,0:T(8,128)S(1)}, ...) custom-call(f32[3,8,64,128]{3,2,1,0:T(8,128)} %vel.1, ...), custom_call_target="tpu_custom_call" | custom-call | tf_op jit(solution)/shard_map/pallas_call | solution.py:751
  15.9 1.4 %shard_map.114 = (f32[5,8,64,128]{3,2,1,0:T(8,128)}, f32[5,1024]{1,0:T(8,128)}) custom-call(f32[5,8,64,128]{3,2,1,0:T(8,128)S(1)} %get-tuple-element.10.part, f32[5,1024]{1,0:T(8,128)S(1)} %get-tuple-element.11.old, f32[2,5,8,128]{3,2,1,0:T(8,128)S(1)} %get-tuple-element.12.dyr, f32[4,8,128]{2,1,0:T(8,128)S(1)} %get-tuple-element.13.dxyr, ...), custom_call_target="tpu_custom_call" | custom-call | tf_op jit(solution)/shard_map/pallas_call | solution.py:761

commit v7 on v6

--- a/solution.py
+++ b/solution.py
@@ -443,6 +443,7 @@
         sample(range(blocks // 2, blocks))
 
     arrive(y_in + xy_in)
+    arrive(z_in + yz_in)
     flat = NUM_FIELDS * ci
     ends = jnp.concatenate(
         [yh[y].reshape(flat, ck) for y in range(2)] + [xyh[q] for q in range(4)], axis=0
@@ -464,7 +465,6 @@
             total += jnp.sum(part, axis=0, keepdims=True) * rim
         sampled[f : f + 1] = total
 
-    arrive(z_in + yz_in)
     lanes = lanes_of((8, 128))
     body = lanes < cj
 

time: 17.6 us -> 17.6 us (level)
  no operation moved by 1% of the time
where the time goes in v7:
time: 17.6 us; the launch traced here: 17.3 us
  Pallas kernels  16 us (91%)
  between operations  1.29 us (7%)
    pallas_call x1, Pallas kernels, local(): pl.pallas_call(functools.partial(kernel, counts), out_shape=results, in_s...  14.6 us
    pallas_call x1, Pallas kernels, local(): pl.pallas_call(finish, out_shape=results[0:2], in_specs=[vmem] * len(resu...  1.39 us

profile of v7, /device:TPU:0, one launch (start us, length us, event | category | flops | bytes accessed | tf_op | source)
XLA Modules:
  0.0 17.3 jit_solution(3979883405731271637)
XLA Ops:
  1.3 14.6 %shard_map.113 = (f32[5,8,64,128]{3,2,1,0:T(8,128)S(1)}, f32[5,1024]{1,0:T(8,128)S(1)}, f32[2,5,8,128]{3,2,1,0:T(8,128)S(1)}, f32[4,8,128]{2,1,0:T(8,128)S(1)}, ...) custom-call(f32[3,8,64,128]{3,2,1,0:T(8,128)} %vel.1, ...), custom_call_target="tpu_custom_call" | custom-call | tf_op jit(solution)/shard_map/pallas_call | solution.py:751
  15.9 1.4 %shard_map.114 = (f32[5,8,64,128]{3,2,1,0:T(8,128)}, f32[5,1024]{1,0:T(8,128)}) custom-call(f32[5,8,64,128]{3,2,1,0:T(8,128)S(1)} %get-tuple-element.10.part, f32[5,1024]{1,0:T(8,128)S(1)} %get-tuple-element.11.old, f32[2,5,8,128]{3,2,1,0:T(8,128)S(1)} %get-tuple-element.12.dyr, f32[4,8,128]{2,1,0:T(8,128)S(1)} %get-tuple-element.13.dxyr, ...), custom_call_target="tpu_custom_call" | custom-call | tf_op jit(solution)/shard_map/pallas_call | solution.py:761

commit v8 on v7

--- a/solution.py
+++ b/solution.py
@@ -561,6 +561,11 @@
         return wide[:, 0:128] + wide[:, 128:256] + nt(low, right[0:128])
 
     shape = (2, NUM_TERMS + 2, ci, 128)
+    fan_hi[1], fan_lo[1] = fan((y_high, y_low))
+    dys[...] = both(fan_hi[1], fan_lo[1], lines[...]).reshape(shape)
+    for message in out:
+        if message.move[2] == 0:
+            message.start()
     fan_hi[0], fan_lo[0] = fan((z_high, z_low))
     dzs[...] = both(fan_hi[0], fan_lo[0], yt[...]).reshape(shape)
     for z in range(2):
@@ -571,11 +576,6 @@
         dyzs[z] = tile
     for message in out:
         if message.move[2] != 0 and 0 in message.move:
-            message.start()
-    fan_hi[1], fan_lo[1] = fan((y_high, y_low))
-    dys[...] = both(fan_hi[1], fan_lo[1], lines[...]).reshape(shape)
-    for message in out:
-        if message.move[2] == 0:
             message.start()
 
     for a in range(0, NUM_TERMS, 2):

time: 17.6 us -> 18.1 us (1.028)
  Pallas kernels: 16 us -> 16.5 us
    pallas_call x1, Pallas kernels: 14.6 us -> 15.1 us  [local(): pl.pallas_call(functools.partial(kernel, counts), out_shape=results, in_s...]
where the time goes in v8:
time: 18.1 us; the launch traced here: 17.8 us
  Pallas kernels  16.5 us (91%)
  between operations  1.29 us (7%)
    pallas_call x1, Pallas kernels, local(): pl.pallas_call(functools.partial(kernel, counts), out_shape=results, in_s...  15.1 us
    pallas_call x1, Pallas kernels, local(): pl.pallas_call(finish, out_shape=results[0:2], in_specs=[vmem] * len(resu...  1.39 us

profile of v8, /device:TPU:0, one launch (start us, length us, event | category | flops | bytes accessed | tf_op | source)
XLA Modules:
  0.0 17.8 jit_solution(12884066089931556819)
XLA Ops:
  1.3 15.1 %shard_map.113 = (f32[5,8,64,128]{3,2,1,0:T(8,128)S(1)}, f32[5,1024]{1,0:T(8,128)S(1)}, f32[2,5,8,128]{3,2,1,0:T(8,128)S(1)}, f32[4,8,128]{2,1,0:T(8,128)S(1)}, ...) custom-call(f32[3,8,64,128]{3,2,1,0:T(8,128)} %vel.1, ...), custom_call_target="tpu_custom_call" | custom-call | tf_op jit(solution)/shard_map/pallas_call | solution.py:751
  16.4 1.4 %shard_map.114 = (f32[5,8,64,128]{3,2,1,0:T(8,128)}, f32[5,1024]{1,0:T(8,128)}) custom-call(f32[5,8,64,128]{3,2,1,0:T(8,128)S(1)} %get-tuple-element.10.part, f32[5,1024]{1,0:T(8,128)S(1)} %get-tuple-element.11.old, f32[2,5,8,128]{3,2,1,0:T(8,128)S(1)} %get-tuple-element.12.dyr, f32[4,8,128]{2,1,0:T(8,128)S(1)} %get-tuple-element.13.dxyr, ...), custom_call_target="tpu_custom_call" | custom-call | tf_op jit(solution)/shard_map/pallas_call | solution.py:761
